TPU v7x, 32 devices: a 4x4x1 block of a 4x4x8 slice. The times are simulated.
32 devices in a mesh: dp: 1 (over z), sx: 4 (over y), sy: 8 (over x, core).
Axes of the slice: x: 4, y: 4, z: 1, core: 2. Of those that a mesh axis runs over, the one named last changes fastest.
The devices are a block of a 4x4x8 slice.
Arguments:
- act_in: bfloat16 [2, 2048, 32, 256], P('dp', 'sy', 'sx')
- norm_first: bfloat16 [2, 256], replicated
- w_first: bfloat16 [3, 3, 256, 128], replicated
- w_short: bfloat16 [256, 128], replicated
- norm_rest: bfloat16 [6, 2, 128], replicated
- w_rest: bfloat16 [5, 3, 3, 128, 128], replicated
- bias_rest: bfloat16 [7, 128], replicated
- w_out: bfloat16 [3, 3, 128, 3], replicated
- bias_out: bfloat16 [3], replicated
Outputs:
- output: float32 [2, 2048, 32, 3], P('dp', 'sy', 'sx')
All inputs are finite; a program needn't handle non-finite values.
Results may differ from a plain program's by a relative error of at most 0.00887721.
Values are sent between devices in bfloat16 or wider.
A program may use at most 768 MiB of HBM per device.

v0:
```python
import jax
import jax.numpy as jnp
from jax import lax
from jax.sharding import PartitionSpec as P

GROUPS = 32
GN_EPS = 1e-6


def solution(mesh):
    rows_n = mesh.shape["sy"]
    cols_n = mesh.shape["sx"]
    to_below = [(position, position + 1) for position in range(rows_n - 1)]
    to_above = [(position + 1, position) for position in range(rows_n - 1)]
    to_right = [(position, position + 1) for position in range(cols_n - 1)]
    to_left = [(position + 1, position) for position in range(cols_n - 1)]
    tile_spec = P("dp", "sy", "sx", None)
    replicated = P()

    def add_border(act_map):
        top_row = lax.ppermute(act_map[:, -1:], "sy", to_below)
        bottom_row = lax.ppermute(act_map[:, :1], "sy", to_above)
        tall = jnp.concatenate([top_row, act_map, bottom_row], axis=1)
        left_col = lax.ppermute(tall[:, :, -1:], "sx", to_right)
        right_col = lax.ppermute(tall[:, :, :1], "sx", to_left)
        return jnp.concatenate([left_col, tall, right_col], axis=2)

    def conv_tile(act_map, kernel):
        return lax.conv_general_dilated(add_border(act_map), kernel, (1, 1), ((0, 0), (0, 0)), dimension_numbers=("NHWC", "HWIO", "NHWC"), preferred_element_type=jnp.float32)

    def group_norm_act(act_map, norm_pair):
        samples = act_map.shape[0]
        per_group = act_map.shape[3] // GROUPS
        group_count = act_map.shape[1] * rows_n * act_map.shape[2] * cols_n * per_group
        sum_one = jnp.sum(act_map, axis=(1, 2), dtype=jnp.float32).reshape(samples, GROUPS, per_group).sum(axis=2)
        sum_two = jnp.sum(jnp.square(act_map.astype(jnp.float32)), axis=(1, 2)).reshape(samples, GROUPS, per_group).sum(axis=2)
        totals = lax.psum(jnp.stack([sum_one, sum_two], axis=-1), ("sy", "sx"))
        group_mean = totals[:, :, 0] / group_count
        inv_std = lax.rsqrt(totals[:, :, 1] / group_count - group_mean * group_mean + GN_EPS)
        chan_scale = jnp.repeat(inv_std, per_group, axis=1) * norm_pair[0].astype(jnp.float32)
        chan_shift = norm_pair[1].astype(jnp.float32) - jnp.repeat(group_mean, per_group, axis=1) * chan_scale
        return jax.nn.silu(act_map.astype(jnp.float32) * chan_scale[:, None, None, :] + chan_shift[:, None, None, :]).astype(jnp.bfloat16)

    def local_decode(act_in, norm_first, w_first, w_short, norm_rest, w_rest, bias_rest, w_out, bias_out):
        bias_rows = bias_rest.astype(jnp.float32)
        mid_act = (conv_tile(group_norm_act(act_in, norm_first), w_first) + bias_rows[0]).astype(jnp.bfloat16)
        skip_path = jnp.einsum("nhwc,cd->nhwd", act_in, w_short, preferred_element_type=jnp.float32) + bias_rows[6]
        hidden = (conv_tile(group_norm_act(mid_act, norm_rest[0]), w_rest[0]) + bias_rows[1] + skip_path).astype(jnp.bfloat16)
        for res_index in range(1, 3):
            first_at = 2 * res_index - 1
            mid_act = (conv_tile(group_norm_act(hidden, norm_rest[first_at]), w_rest[first_at]) + bias_rows[first_at + 1]).astype(jnp.bfloat16)
            hidden = (conv_tile(group_norm_act(mid_act, norm_rest[first_at + 1]), w_rest[first_at + 1]) + bias_rows[first_at + 2] + hidden.astype(jnp.float32)).astype(jnp.bfloat16)
        return conv_tile(group_norm_act(hidden, norm_rest[5]), w_out) + bias_out.astype(jnp.float32)

    return jax.shard_map(local_decode, mesh=mesh, in_specs=(tile_spec, replicated, replicated, replicated, replicated, replicated, replicated, replicated, replicated), out_specs=tile_spec, check_vma=False)
```

profile of v0, /device:TPU:97, one launch (start us, length us, event | category | flops | bytes accessed | tf_op | source)
XLA Modules:
  0.0 532.5 jit_solution(1492962058845114028)
XLA Ops:
  0.0 5.9 %convert_reduce_fusion = (f32[2,256]{1,0:T(2,128)S(1)}, f32[2,256]{1,0:T(2,128)S(1)}) fusion(bf16[2,256,8,256]{3,2,1,0:T(8,128)(2,1)} %param.9), kind=kLoop, calls=%fused_computation.2 | loop fusion | flops 4193280 | bytes 2101248 | tf_op jit(solution)/shard_map/reduce_sum | solution.py:35
  6.3 49.8 %psum.49 = f32[2,32,2]{1,0,2:T(2,128)S(1)} all-reduce(f32[2,32,2]{1,0,2:T(2,128)S(1)} %pad_maximum_fusion.39), channel_id=1, replica_groups=mesh['dp'=1,'sx'=4,'sy'=8] {'sy','sx'}, use_global_device_ids=true, to_apply=%region_4.0 | all-reduce | flops 128 | bytes 1024 | tf_op jit(solution)/shard_map/psum | solution.py:37
  56.6 6.9 %fusion.2 = bf16[2,256,8,256]{3,0,2,1:T(2,128)(2,1)S(1)} fusion(f32[2,256]{1,0:T(2,128)S(1)} %get-tuple-element.31, f32[2,256]{1,0:T(2,128)S(1)} %get-tuple-element.32, bf16[2,256,8,256]{3,2,1,0:T(8,128)(2,1)S(1)} %copy-done.1), kind=kLoop, calls=%fused_computation.6 | loop fusion | flops 8388608 | bytes 4198400 | tf_op jit(solution)/shard_map/convert_element_type | solution.py:42
  65.5 2.4 collective-permute-start.1
  68.0 2.5 collective-permute-done.1
  71.3 2.4 collective-permute-start.2
  75.6 2.8 collective-permute-done.2
  78.4 4.2 collective-permute-done.3
  82.6 12.4 %convert_reduce_fusion.6 = (f32[2,128]{1,0:T(2,128)S(1)}, f32[2,128]{1,0:T(2,128)S(1)}, bf16[2,256,8,128]{3,0,2,1:T(2,128)(2,1)}) fusion(f32[128]{0:T(128)S(1)} %get-tuple-element.67, bf16[3,3,256,128]{3,2,1,0:T(8,128)(2,1)S(1)} %copy-done, bf16[2,258,1,256]{3,0,2,1:T(2,128)(2,1)S(1)} %collective-permute-done.3, ...), kind=kOutput, calls=%fused_computation.26 | convolution fusion | flops 2432273920 | bytes 4282880 | tf_op jit(solution)/shard_map/conv_general_dilated | solution.py:29
  95.4 45.1 %psum.50 = f32[2,32,2]{1,0,2:T(2,128)S(1)} all-reduce(f32[2,32,2]{1,0,2:T(2,128)S(1)} %pad_maximum_fusion.40), channel_id=1, replica_groups=mesh['dp'=1,'sx'=4,'sy'=8] {'sy','sx'}, use_global_device_ids=true, to_apply=%region_9.10 | all-reduce | flops 128 | bytes 1024 | tf_op jit(solution)/shard_map/psum | solution.py:37
  140.9 3.5 fusion.25
  144.5 2.3 collective-permute-start.4
  148.9 2.8 collective-permute-done.5
  156.1 4.0 collective-permute-done.7
  160.1 9.0 %convert_reduce_fusion.2 = (f32[2,128]{1,0:T(2,128)S(1)}, f32[2,128]{1,0:T(2,128)S(1)}, bf16[2,256,8,128]{3,0,2,1:T(2,128)(2,1)S(1)}) fusion(f32[128]{0:T(128)S(1)} %get-tuple-element.65, f32[2,256,8,128]{3,2,1,0:T(8,128)S(1)} %fusion.63, f32[128]{0:T(128)S(1)} %get-tuple-element.66, bf16[5,3,3,128,128]{4,3,2,1,0:T(8,128)(2,1)} %param.14, ...), kind=kOutput, calls=%fused_computation.14 | convolution fusion | flops 1218758144 | bytes 4764672 | tf_op jit(solution)/shard_map/conv_general_dilated | solution.py:29
  169.6 45.6 %psum.51 = f32[2,32,2]{1,0,2:T(2,128)S(1)} all-reduce(f32[2,32,2]{1,0,2:T(2,128)S(1)} %pad_maximum_fusion.41), channel_id=1, replica_groups=mesh['dp'=1,'sx'=4,'sy'=8] {'sy','sx'}, use_global_device_ids=true, to_apply=%region_14.15 | all-reduce | flops 128 | bytes 1024 | tf_op jit(solution)/shard_map/psum | solution.py:37
  215.6 2.5 fusion.24
  220.3 2.2 collective-permute-start.9
  222.5 2.7 collective-permute-done.9
  225.6 2.2 collective-permute-start.10
  229.8 4.1 collective-permute-done.11
  233.9 7.8 %convert_reduce_fusion.5 = (f32[2,128]{1,0:T(2,128)S(1)}, f32[2,128]{1,0:T(2,128)S(1)}, bf16[2,256,8,128]{3,0,2,1:T(2,128)(2,1)S(1)}) fusion(f32[128]{0:T(128)S(1)} %get-tuple-element.64, bf16[5,3,3,128,128]{4,3,2,1,0:T(8,128)(2,1)} %param.14, bf16[2,258,1,128]{3,0,2,1:T(2,128)(2,1)S(1)} %collective-permute-done.11, ...), kind=kOutput, calls=%fused_computation.23 | convolution fusion | flops 1217709568 | bytes 2667008 | tf_op jit(solution)/shard_map/conv_general_dilated | solution.py:29
  242.1 45.3 %psum.52 = f32[2,32,2]{1,0,2:T(2,128)S(1)} all-reduce(f32[2,32,2]{1,0,2:T(2,128)S(1)} %pad_maximum_fusion.42), channel_id=1, replica_groups=mesh['dp'=1,'sx'=4,'sy'=8] {'sy','sx'}, use_global_device_ids=true, to_apply=%region_19.20 | all-reduce | flops 128 | bytes 1024 | tf_op jit(solution)/shard_map/psum | solution.py:37
  287.8 2.5 fusion.23
  292.5 2.2 collective-permute-start.13
  294.7 2.7 collective-permute-done.13
  302.0 4.1 collective-permute-done.15
  306.1 8.7 %convert_reduce_fusion.1 = (f32[2,128]{1,0:T(2,128)S(1)}, f32[2,128]{1,0:T(2,128)S(1)}, bf16[2,256,8,128]{3,0,2,1:T(2,128)(2,1)S(1)}) fusion(bf16[2,256,8,128]{3,0,2,1:T(2,128)(2,1)S(1)} %get-tuple-element.83, f32[128]{0:T(128)S(1)} %get-tuple-element.63, bf16[5,3,3,128,128]{4,3,2,1,0:T(8,128)(2,1)} %param.14, ...), kind=kOutput, calls=%fused_computation.10 | convolution fusion | flops 1218758144 | bytes 3715584 | tf_op jit(solution)/shard_map/conv_general_dilated | solution.py:29
  315.2 45.5 %psum.53 = f32[2,32,2]{1,0,2:T(2,128)S(1)} all-reduce(f32[2,32,2]{1,0,2:T(2,128)S(1)} %pad_maximum_fusion.43), channel_id=1, replica_groups=mesh['dp'=1,'sx'=4,'sy'=8] {'sy','sx'}, use_global_device_ids=true, to_apply=%region_24.25 | all-reduce | flops 128 | bytes 1024 | tf_op jit(solution)/shard_map/psum | solution.py:37
  361.1 2.5 fusion.22
  365.8 2.2 collective-permute-start.17
  368.0 2.7 collective-permute-done.17
  371.1 2.2 collective-permute-start.18
  375.3 4.1 collective-permute-done.19
  379.4 7.9 %convert_reduce_fusion.4 = (f32[2,128]{1,0:T(2,128)S(1)}, f32[2,128]{1,0:T(2,128)S(1)}, bf16[2,256,8,128]{3,0,2,1:T(2,128)(2,1)S(1)}) fusion(f32[128]{0:T(128)S(1)} %get-tuple-element.62, bf16[5,3,3,128,128]{4,3,2,1,0:T(8,128)(2,1)} %param.14, bf16[2,258,1,128]{3,0,2,1:T(2,128)(2,1)S(1)} %collective-permute-done.19, ...), kind=kOutput, calls=%fused_computation.20 | convolution fusion | flops 1217709568 | bytes 2667008 | tf_op jit(solution)/shard_map/conv_general_dilated | solution.py:29
  387.7 45.3 %psum.54 = f32[2,32,2]{1,0,2:T(2,128)S(1)} all-reduce(f32[2,32,2]{1,0,2:T(2,128)S(1)} %pad_maximum_fusion.44), channel_id=1, replica_groups=mesh['dp'=1,'sx'=4,'sy'=8] {'sy','sx'}, use_global_device_ids=true, to_apply=%region_29.30 | all-reduce | flops 128 | bytes 1024 | tf_op jit(solution)/shard_map/psum | solution.py:37
  433.4 2.5 fusion.21
  438.1 2.2 collective-permute-start.21
  440.3 2.7 collective-permute-done.21
  447.6 4.1 collective-permute-done.23
  451.7 8.7 %convert_reduce_fusion.3 = (f32[2,128]{1,0:T(2,128)S(1)}, f32[2,128]{1,0:T(2,128)S(1)}, bf16[2,256,8,128]{3,0,2,1:T(2,128)(2,1)S(1)}) fusion(bf16[2,256,8,128]{3,0,2,1:T(2,128)(2,1)S(1)} %get-tuple-element.85, f32[128]{0:T(128)S(1)} %get-tuple-element.61, bf16[5,3,3,128,128]{4,3,2,1,0:T(8,128)(2,1)} %param.14, ...), kind=kOutput, calls=%fused_computation.17 | convolution fusion | flops 1218758144 | bytes 3715584 | tf_op jit(solution)/shard_map/conv_general_dilated | solution.py:29
  460.8 45.5 %psum.55 = f32[2,32,2]{1,0,2:T(2,128)S(1)} all-reduce(f32[2,32,2]{1,0,2:T(2,128)S(1)} %pad_maximum_fusion.45), channel_id=1, replica_groups=mesh['dp'=1,'sx'=4,'sy'=8] {'sy','sx'}, use_global_device_ids=true, to_apply=%region_34.35 | all-reduce | flops 128 | bytes 1024 | tf_op jit(solution)/shard_map/psum | solution.py:37
  506.7 2.5 fusion.20
  511.4 2.2 collective-permute-start.25
  513.7 2.7 collective-permute-done.25
  516.8 2.2 collective-permute-start.26
  520.9 4.1 collective-permute-done.27
  525.1 5.5 %fusion.62 = f32[2,256,8,3]{3,0,2,1:T(2,128)S(1)} fusion(bf16[3,3,128,3]{2,3,1,0:T(4,128)(2,1)S(1)} %copy-done.6, bf16[2,258,1,128]{3,0,2,1:T(2,128)(2,1)S(1)} %collective-permute-done.27, bf16[2,1,8,128]{3,0,2,1:T(2,128)(2,1)S(1)} %collective-permute-done.25, bf16[2,256,8,128]{3,0,2,1:T(2,128)(2,1)S(1)} %fusion.20, ...), kind=kOutput, calls=%fused_computation.103 | convolution fusion | flops 34928640 | bytes 1377036 | tf_op jit(solution)/shard_map/conv_general_dilated | solution.py:29
  (151 shorter events, 44.9 us)
Async XLA Ops:
  0.0 82.6 %copy-start = (bf16[3,3,256,128]{3,2,1,0:T(8,128)(2,1)S(1)}, bf16[3,3,256,128]{3,2,1,0:T(8,128)(2,1)}, u32[]{:S(2)}) copy-start(bf16[3,3,256,128]{3,2,1,0:T(8,128)(2,1)} %param.11) | copy-start | bytes 1769476
  0.0 56.5 %copy-start.1 = (bf16[2,256,8,256]{3,2,1,0:T(8,128)(2,1)S(1)}, bf16[2,256,8,256]{3,2,1,0:T(8,128)(2,1)}, u32[]{:S(2)}) copy-start(bf16[2,256,8,256]{3,2,1,0:T(8,128)(2,1)} %param.9) | copy-start | bytes 6291460
  0.0 56.5 %copy-start.4 = (bf16[2,256]{1,0:T(2,128)(2,1)S(1)}, bf16[2,256]{1,0:T(2,128)(2,1)}, u32[]{:S(2)}) copy-start(bf16[2,256]{1,0:T(2,128)(2,1)} %param.10) | copy-start | bytes 3076
  63.5 12.1 %copy-start.3 = (bf16[6,2,128]{2,1,0:T(2,128)(2,1)S(1)}, bf16[6,2,128]{2,1,0:T(2,128)(2,1)}, u32[]{:S(2)}) copy-start(bf16[6,2,128]{2,1,0:T(2,128)(2,1)} %param.13) | copy-start | bytes 9220
  63.5 12.1 %copy-start.5 = (bf16[7,128]{1,0:T(8,128)(2,1)S(1)}, bf16[7,128]{1,0:T(8,128)(2,1)}, u32[]{:S(2)}) copy-start(bf16[7,128]{1,0:T(8,128)(2,1)} %param.15) | copy-start | bytes 5380
  63.5 4.4 collective-permute-start
  65.5 5.0 collective-permute-start.1
  71.3 7.1 %collective-permute-start.2 = (bf16[2,258,1,256]{3,0,2,1:T(2,128)(2,1)S(1)}, bf16[2,258,1,256]{3,0,2,1:T(2,128)(2,1)S(1)}, u32[]{:S(2)}, u32[]{:S(2)}) collective-permute-start(bf16[2,258,1,256]{3,0,2,1:T(2,128)(2,1)S(1)} %get-tuple-element.33), channel_id=1, source_target_pairs={{0,8},{8,16},{16,24},{1,9},{9,17},{17,25},{2,10},{10,18},{18,26},{... | collective-permute-start | bytes 792584 | tf_op jit(solution)/shard_map/ppermute | solution.py:24
  73.7 8.8 %collective-permute-start.3 = (bf16[2,258,1,256]{3,0,2,1:T(2,128)(2,1)S(1)}, bf16[2,258,1,256]{3,0,2,1:T(2,128)(2,1)S(1)}, u32[]{:S(2)}, u32[]{:S(2)}) collective-permute-start(bf16[2,258,1,256]{3,0,2,1:T(2,128)(2,1)S(1)} %get-tuple-element.34), channel_id=1, source_target_pairs={{8,0},{16,8},{24,16},{9,1},{17,9},{25,17},{10,2},{18,10},{26,18},{... | collective-permute-start | bytes 792584 | tf_op jit(solution)/shard_map/ppermute | solution.py:25
  95.0 60.4 %copy-start.2 = (bf16[256,128]{1,0:T(8,128)(2,1)S(1)}, bf16[256,128]{1,0:T(8,128)(2,1)}, u32[]{:S(2)}) copy-start(bf16[256,128]{1,0:T(8,128)(2,1)} %param.12) | copy-start | bytes 196612
  144.5 4.4 collective-permute-start.4
  146.7 5.0 collective-permute-start.5
  152.1 4.0 collective-permute-start.6
  154.1 6.1 %collective-permute-start.7 = (bf16[2,258,1,128]{3,0,2,1:T(2,128)(2,1)S(1)}, bf16[2,258,1,128]{3,0,2,1:T(2,128)(2,1)S(1)}, u32[]{:S(2)}, u32[]{:S(2)}) collective-permute-start(bf16[2,258,1,128]{3,0,2,1:T(2,128)(2,1)S(1)} %get-tuple-element.48), channel_id=1, source_target_pairs={{8,0},{16,8},{24,16},{9,1},{17,9},{25,17},{10,2},{18,10},{26,18},{... | collective-permute-start | bytes 396296 | tf_op jit(solution)/shard_map/ppermute | solution.py:25
  218.1 4.4 collective-permute-start.8
  220.3 5.0 collective-permute-start.9
  225.6 4.2 collective-permute-start.10
  227.8 6.1 %collective-permute-start.11 = (bf16[2,258,1,128]{3,0,2,1:T(2,128)(2,1)S(1)}, bf16[2,258,1,128]{3,0,2,1:T(2,128)(2,1)S(1)}, u32[]{:S(2)}, u32[]{:S(2)}) collective-permute-start(bf16[2,258,1,128]{3,0,2,1:T(2,128)(2,1)S(1)} %get-tuple-element.46), channel_id=1, source_target_pairs={{8,0},{16,8},{24,16},{9,1},{17,9},{25,17},{10,2},{18,10},{26,18},{... | collective-permute-start | bytes 396296 | tf_op jit(solution)/shard_map/ppermute | solution.py:25
  290.3 4.4 collective-permute-start.12
  292.5 5.0 collective-permute-start.13
  297.9 4.2 collective-permute-start.14
  300.1 6.1 %collective-permute-start.15 = (bf16[2,258,1,128]{3,0,2,1:T(2,128)(2,1)S(1)}, bf16[2,258,1,128]{3,0,2,1:T(2,128)(2,1)S(1)}, u32[]{:S(2)}, u32[]{:S(2)}) collective-permute-start(bf16[2,258,1,128]{3,0,2,1:T(2,128)(2,1)S(1)} %get-tuple-element.44), channel_id=1, source_target_pairs={{8,0},{16,8},{24,16},{9,1},{17,9},{25,17},{10,2},{18,10},{26,18},{... | collective-permute-start | bytes 396296 | tf_op jit(solution)/shard_map/ppermute | solution.py:25
  363.6 4.4 collective-permute-start.16
  365.8 5.0 collective-permute-start.17
  371.1 4.2 collective-permute-start.18
  373.4 6.1 %collective-permute-start.19 = (bf16[2,258,1,128]{3,0,2,1:T(2,128)(2,1)S(1)}, bf16[2,258,1,128]{3,0,2,1:T(2,128)(2,1)S(1)}, u32[]{:S(2)}, u32[]{:S(2)}) collective-permute-start(bf16[2,258,1,128]{3,0,2,1:T(2,128)(2,1)S(1)} %get-tuple-element.42), channel_id=1, source_target_pairs={{8,0},{16,8},{24,16},{9,1},{17,9},{25,17},{10,2},{18,10},{26,18},{... | collective-permute-start | bytes 396296 | tf_op jit(solution)/shard_map/ppermute | solution.py:25
  435.9 4.4 collective-permute-start.20
  438.1 5.0 collective-permute-start.21
  443.4 4.2 collective-permute-start.22
  445.6 6.1 %collective-permute-start.23 = (bf16[2,258,1,128]{3,0,2,1:T(2,128)(2,1)S(1)}, bf16[2,258,1,128]{3,0,2,1:T(2,128)(2,1)S(1)}, u32[]{:S(2)}, u32[]{:S(2)}) collective-permute-start(bf16[2,258,1,128]{3,0,2,1:T(2,128)(2,1)S(1)} %get-tuple-element.40), channel_id=1, source_target_pairs={{8,0},{16,8},{24,16},{9,1},{17,9},{25,17},{10,2},{18,10},{26,18},{... | collective-permute-start | bytes 396296 | tf_op jit(solution)/shard_map/ppermute | solution.py:25
  460.4 59.9 %copy-start.7 = (bf16[3]{0:T(256)(128)(2,1)S(1)}, bf16[3]{0:T(256)(128)(2,1)}, u32[]{:S(2)}) copy-start(bf16[3]{0:T(256)(128)(2,1)} %param.17) | copy-start | bytes 22
  460.4 64.7 %copy-start.6 = (bf16[3,3,128,3]{2,3,1,0:T(4,128)(2,1)S(1)}, bf16[3,3,128,3]{2,3,1,0:T(4,128)(2,1)}, u32[]{:S(2)}) copy-start(bf16[3,3,128,3]{2,3,1,0:T(4,128)(2,1)} %param.16) | copy-start | bytes 20740
  509.3 4.4 collective-permute-start.24
  511.4 5.0 collective-permute-start.25
  516.8 4.2 collective-permute-start.26
  519.0 6.1 %collective-permute-start.27 = (bf16[2,258,1,128]{3,0,2,1:T(2,128)(2,1)S(1)}, bf16[2,258,1,128]{3,0,2,1:T(2,128)(2,1)S(1)}, u32[]{:S(2)}, u32[]{:S(2)}) collective-permute-start(bf16[2,258,1,128]{3,0,2,1:T(2,128)(2,1)S(1)} %get-tuple-element.38), channel_id=1, source_target_pairs={{8,0},{16,8},{24,16},{9,1},{17,9},{25,17},{10,2},{18,10},{26,18},{... | collective-permute-start | bytes 396296 | tf_op jit(solution)/shard_map/ppermute | solution.py:25
where the time goes:
time: 541 us; the launch traced here: 533 us
  blocking collectives  322 us (60%)
  matrix products  60.6 us (11%)
  starting transfers between devices  55.9 us (10%)
  waiting for transfers between devices  53.6 us (10%)
  other arithmetic  33.4 us (6%)
  local copies, waits for them, and re-layouts  5.66 us (1%)
    psum x7, blocking collectives, group_norm_act(): totals = lax.psum(jnp.stack([sum_one, sum_two], axis=-1), ('sy', 'sx'))  322 us
    conv_general_dilated x7, matrix products, conv_tile(): lax.conv_general_dilated(add_border(act_map), kernel, (1, 1), ((0, 0), (0...  59.9 us
    ppermute x7, waiting for transfers between devices, add_border(): right_col = lax.ppermute(tall[:, :, :1], 'sx', to_left)  28.8 us
    convert_element_type x7, other arithmetic, group_norm_act(): jax.nn.silu(act_map.astype(jnp.float32) * chan_scale[:, None, None, :] +...  23 us
    ppermute x7, waiting for transfers between devices, add_border(): bottom_row = lax.ppermute(act_map[:, :1], 'sy', to_above)  18.9 us
    ppermute x7, starting transfers between devices, add_border(): bottom_row = lax.ppermute(act_map[:, :1], 'sy', to_above)  15.7 us
    ppermute x7, starting transfers between devices, add_border(): left_col = lax.ppermute(tall[:, :, -1:], 'sx', to_right)  15.6 us
    ppermute x7, starting transfers between devices, add_border(): top_row = lax.ppermute(act_map[:, -1:], 'sy', to_below)  15 us
  transfers between devices with their start and end apart: 28, of which 20 were waited for; matrix products, arithmetic and copies ran while one was open for 0% of the time, Pallas kernels for 0%

commit v1 on v0

v1 whole, which is shorter than its diff:
```python
import functools

import jax
import jax.numpy as jnp
from jax import lax
from jax.experimental import pallas as pl
from jax.experimental.pallas import tpu as pltpu
from jax.sharding import PartitionSpec as P

GROUPS = 32
GN_EPS = 1e-6
LANES = 128
MESH = pl.DeviceIdType.MESH
F32 = jnp.float32
BF16 = jnp.bfloat16


def half_silu(half):
    return half + half * jnp.tanh(half)


def decode_kernel(rows_n, cols_n, act_hbm, w_first_hbm, w_short_hbm, w_rest_hbm, norm_first_ref, norm_rest_ref, bias_ref, w_out_ref, out_ref,
                  raw, flat, map_in, maps, sh, z_in, z_mid, short, w_first, w_short, w_rest, w_head, ones_in, ones_mid,
                  msg_in, msg_mid, got_in, got_mid, edge_in, edge_mid, halo_in, halo_mid,
                  act_sem, weight_sem, stat_recv, stat_send, halo_recv, halo_send):
    samples, rows, cols, in_ch = raw.shape
    halves = in_ch // LANES
    layers = w_rest.shape[0] + 1
    peers_n = rows_n * cols_n - 1
    sx = lax.axis_index("sx")
    sy = lax.axis_index("sy")
    core = lax.rem(sy, 2)
    chip = sy // 2
    chips_n = rows_n // 2

    def ring(offset, size):
        return min(offset, size - offset)

    offsets = [(dx, dy, dc) for dx in range(cols_n) for dy in range(chips_n) for dc in range(2) if (dx, dy, dc) != (0, 0, 0)]
    offsets.sort(key=lambda o: (-ring(o[0], cols_n) - ring(o[1], chips_n), -o[2]))

    def peer(offset):
        dx, dy, dc = offset
        return {"sx": lax.rem(sx + dx, cols_n), "sy": lax.rem(chip + dy, chips_n) * 2 + lax.rem(core + dc, 2)}

    for s in range(samples):
        pltpu.make_async_copy(act_hbm.at[s], raw.at[s], act_sem.at[s]).start()
    for o in range(2):
        for dc in range(3):
            pltpu.make_async_copy(w_first_hbm.at[:, dc], w_first.at[o + dc, :, :, pl.ds(o * LANES, LANES)], weight_sem.at[0]).start()
    pltpu.make_async_copy(w_short_hbm, w_short, weight_sem.at[layers]).start()
    for k in range(layers - 1):
        for o in range(2):
            for dc in range(3):
                pltpu.make_async_copy(w_rest_hbm.at[k, :, dc], w_rest.at[k, o + dc, :, :, pl.ds(o * LANES, LANES)], weight_sem.at[k + 1]).start()

    barrier = pltpu.get_barrier_semaphore()
    for offset in offsets:
        pl.semaphore_signal(barrier, inc=1, device_id=peer(offset), device_id_type=MESH)

    row_id = lax.broadcasted_iota(jnp.int32, (LANES, LANES), 0)
    lane_id = lax.broadcasted_iota(jnp.int32, (LANES, LANES), 1)
    for ones, per_group in ((ones_in, in_ch // GROUPS), (ones_mid, LANES // GROUPS)):
        ones[...] = jnp.where(row_id // per_group == lane_id // per_group, 1.0, 0.0).astype(F32)
    for dr in range(3):
        w_first[3, dr, :, 0:LANES] = jnp.zeros((in_ch, LANES), BF16)
        w_first[0, dr, :, LANES:] = jnp.zeros((in_ch, LANES), BF16)

        def clear(k, _):
            w_rest[k, 3, dr, :, 0:LANES] = jnp.zeros((LANES, LANES), BF16)
            w_rest[k, 0, dr, :, LANES:] = jnp.zeros((LANES, LANES), BF16)
            return 0

        lax.fori_loop(0, layers - 1, clear, 0)

    @pl.when(sx == 0)
    def _():
        z_in[:, 0:3 * in_ch] = jnp.zeros((rows, 3 * in_ch), BF16)
        z_mid[:, 0:3 * LANES] = jnp.zeros((rows, 3 * LANES), BF16)

    @pl.when(sx == cols_n - 1)
    def _():
        z_in[:, (cols + 1) * 3 * in_ch:] = jnp.zeros((rows, 3 * in_ch), BF16)
        z_mid[:, (cols + 1) * 3 * LANES:] = jnp.zeros((rows, 3 * LANES), BF16)

    has = {"up": sy > 0, "down": sy < rows_n - 1, "left": sx > 0, "right": sx < cols_n - 1}

    def both(one, two):
        return jnp.logical_and(has[one], has[two])

    row_moves = [
        (1, 1, 0, {"sy": sy - 1}, has["up"], has["down"]),
        (0, 1, 1, {"sy": sy + 1}, has["down"], has["up"]),
        (1, 2, 0, {"sx": sx - 1, "sy": sy - 1}, both("up", "left"), both("down", "right")),
        (1, 0, 0, {"sx": sx + 1, "sy": sy - 1}, both("up", "right"), both("down", "left")),
        (0, 2, 1, {"sx": sx - 1, "sy": sy + 1}, both("down", "left"), both("up", "right")),
        (0, 0, 1, {"sx": sx + 1, "sy": sy + 1}, both("down", "right"), both("up", "left")),
    ]

    def tile(k, s, c):
        return map_in.at[s, c] if k == 0 else maps.at[k - 1, s, c]

    def edges(k, s):
        return edge_in.at[s] if k == 0 else edge_mid.at[k - 1, s]

    def halo(k, s):
        return halo_in.at[s] if k == 0 else halo_mid.at[k - 1, s]

    def message(k, s):
        return msg_in.at[s] if k == 0 else msg_mid.at[k - 1, s]

    def received(k, s):
        return got_in.at[s] if k == 0 else got_mid.at[k - 1, s]

    def col_copy(k, s, at):
        src, dst, to = ((1, cols + 1, {"sx": sx - 1}), (cols, 0, {"sx": sx + 1}))[at]
        return pltpu.make_async_remote_copy(tile(k, s, src), tile(k, s, dst), halo_send.at[k, s, at], halo_recv.at[k, s, at], device_id=to, device_id_type=MESH)

    def row_copy(k, s, at):
        side, place, edge, to, _, _ = row_moves[at]
        return pltpu.make_async_remote_copy(edges(k, s).at[edge], halo(k, s).at[side, place], halo_send.at[k, s, 2 + at], halo_recv.at[k, s, 2 + at], device_id=to, device_id_type=MESH)

    def send_cols(k, s):
        for at, there in enumerate((has["left"], has["right"])):
            pl.when(there)(lambda at=at: col_copy(k, s, at).start())

    def send_rows(k, s):
        for at, move in enumerate(row_moves):
            pl.when(move[4])(lambda at=at: row_copy(k, s, at).start())

    def send_stats(k, s):
        for slot, offset in enumerate(offsets):
            pltpu.make_async_remote_copy(message(k, s), received(k, s).at[slot], stat_send.at[k, s], stat_recv.at[k, s], device_id=peer(offset), device_id_type=MESH).start()

    def wait_rows(k, s):
        for at, move in enumerate(row_moves):
            pl.when(move[5])(lambda at=at: row_copy(k, s, at).wait_recv())

    def store_stats(k, s, sums):
        target = message(k, s)
        for at, part in enumerate(sums):
            target[at:at + 1, :] = jnp.sum(part, axis=0, keepdims=True)

    def scales(k, s):
        pltpu.make_async_copy(received(k, s), received(k, s), stat_recv.at[k, s]).wait()
        total = message(k, s)[...] + jnp.sum(received(k, s)[...], axis=0)
        ones = ones_in if k == 0 else ones_mid
        total = jnp.dot(total, ones[...], precision=lax.Precision.HIGHEST, preferred_element_type=F32)
        parts = halves if k == 0 else 1
        per_group = parts * LANES // GROUPS
        count = rows * rows_n * cols * cols_n * per_group
        rows_out = []
        for part in range(parts):
            norm = (norm_first_ref[:, part * LANES:(part + 1) * LANES] if k == 0 else norm_rest_ref[k - 1]).astype(F32)
            mean = total[part:part + 1] / count
            square = total[parts + part:parts + part + 1] / count
            scale = lax.rsqrt(square - mean * mean + GN_EPS) * norm[0:1]
            shift = norm[1:2] - mean * scale
            rows_out.append((0.5 * scale, 0.5 * shift))
        return rows_out

    def activate(k, s):
        z = z_in if k == 0 else z_mid
        parts = halves if k == 0 else 1
        scale_rows = scales(k, s)
        wait_rows(k, s)
        for part, (scale, shift) in enumerate(scale_rows):
            for side, there in ((0, "up"), (1, "down")):
                at_row = 7 if side == 0 else 8 + rows
                for place in range(3):
                    source = halo(k, s)[side, place, part]
                    seen = has[there] if place == 1 else both(there, "left" if place == 0 else "right")
                    act = jnp.where(seen, half_silu(source * scale + shift), 0.0)
                    for c in ((0,), range(1, cols + 1), (cols + 1,))[place]:
                        pick = (c + cols - 1) % cols
                        sh[part, c, at_row:at_row + 1, :] = act[pick:pick + 1]

        def column(c):
            for part, (scale, shift) in enumerate(scale_rows):
                ref = map_in.at[s, c, part] if k == 0 else maps.at[k - 1, s, c]
                act = half_silu(ref[...].astype(F32) * scale + shift)
                sh[part, c, 8:8 + rows, :] = act
                for dr in range(3):
                    at = c * 3 * parts * LANES + (dr * parts + part) * LANES
                    z[:, pl.ds(pl.multiple_of(at, LANES), LANES)] = (act if dr == 1 else sh[part, c, 7 + dr:7 + dr + rows, :]).astype(BF16)

        lax.fori_loop(1, cols + 1, lambda c, _: (column(c), 0)[1], 0)
        for at, (there, c) in enumerate((("right", cols + 1), ("left", 0))):

            @pl.when(has[there])
            def _(at=at, c=c):
                col_copy(k, s, at).wait_recv()
                column(c)

    def convolve(k, s):
        z = z_in if k == 0 else z_mid
        depth = 3 * (halves if k == 0 else 1) * LANES
        weights = (w_first[...] if k == 0 else w_rest[k - 1]).reshape(4 * depth, 2 * LANES)
        bias = bias_ref[k:k + 1].astype(F32)
        edge = edges(k + 1, s)

        def pair(p, sums):
            lhs = z[:, pl.ds(pl.multiple_of(p * 2 * depth, LANES), 4 * depth)]
            acc = jnp.dot(lhs, weights, preferred_element_type=F32)
            sum_one, sum_two = sums
            for o in range(2):
                c = 2 * p + o
                value = acc[:, o * LANES:(o + 1) * LANES] + bias
                if k == 1:
                    value = value + short[s, c]
                elif k > 1 and k % 2 == 1:
                    value = value + maps[k - 2, s, c + 1].astype(F32)
                rounded = value.astype(BF16)
                maps[k, s, c + 1] = rounded
                value = rounded.astype(F32)
                edge[0, 0, pl.ds(c, 1), :] = value[0:1]
                edge[1, 0, pl.ds(c, 1), :] = value[rows - 1:rows]
                value = value.reshape(rows // 8, 8, LANES)
                sum_one = sum_one + jnp.sum(value, axis=0)
                sum_two = sum_two + jnp.sum(value * value, axis=0)
            return sum_one, sum_two

        zero = jnp.zeros((8, LANES), F32)
        outer = cols // 2 - 1
        sums = lax.fori_loop(0, 2, lambda i, acc: pair(i * outer, acc), (zero, zero))
        send_cols(k + 1, s)
        sums = lax.fori_loop(1, outer, pair, sums)
        store_stats(k + 1, s, sums)
        send_rows(k + 1, s)
        send_stats(k + 1, s)

    chunk = 16

    def load(s):
        pltpu.make_async_copy(act_hbm.at[s], raw.at[s], act_sem.at[s]).wait()

        def step(i, sums):
            at = pl.multiple_of(i * chunk, chunk)
            sums = list(sums)
            for part in range(halves):
                value = raw[s, pl.ds(at, chunk), :, part * LANES:(part + 1) * LANES].astype(F32)
                flat[s, part, pl.ds(pl.multiple_of(at * cols, chunk * cols), chunk * cols), :] = value.reshape(chunk * cols, LANES)
                sums[part] = sums[part] + jnp.sum(value, axis=0)
                sums[halves + part] = sums[halves + part] + jnp.sum(value * value, axis=0)
            return tuple(sums)

        zero = jnp.zeros((cols, LANES), F32)
        sums = lax.fori_loop(0, rows // chunk, step, (zero,) * (2 * halves))
        store_stats(0, s, sums)
        for part in range(halves):
            edge_in[s, 0, part] = flat[s, part, 0:cols, :]
            edge_in[s, 1, part] = flat[s, part, (rows - 1) * cols:, :]

    def turn(s, c):
        for part in range(halves):
            map_in[s, c + 1, part] = flat[s, part, pl.ds(c, rows, stride=cols), :].astype(BF16)

    for s in range(samples):
        load(s)
        turn(s, 0)
        turn(s, cols - 1)
        if s == 0:
            pl.semaphore_wait(barrier, peers_n)
        send_rows(0, s)
        send_stats(0, s)
        send_cols(0, s)
    for s in range(samples):
        for c in range(1, cols - 1):
            turn(s, c)

    col_id = lax.broadcasted_iota(jnp.int32, (cols, LANES), 0)
    for j in range(cols + 2):
        for dr in range(3):
            blocks = []
            for ch in range(3):
                block = jnp.zeros((cols, LANES), F32)
                for dc in range(3):
                    block = jnp.where(col_id == j - dc, w_out_ref[dr, dc, ch:ch + 1, :].astype(F32), block)
                blocks.append(block)
            blocks.append(jnp.zeros((cols, LANES), F32))
            at = (j * 3 + dr) * LANES
            w_head[:, at:at + LANES] = jnp.concatenate(blocks, axis=0).astype(BF16)

    for k in range(layers):
        if k == 0:
            pltpu.make_async_copy(w_first.at[0:3], w_first.at[0:3], weight_sem.at[0]).wait()
        else:
            pltpu.make_async_copy(w_rest.at[k - 1, 0:3], w_rest.at[k - 1, 0:3], weight_sem.at[k]).wait()
        for s in range(samples):
            activate(k, s)
            convolve(k, s)
        if k == 0:
            pltpu.make_async_copy(w_short_hbm, w_short, weight_sem.at[layers]).wait()
            skip_bias = bias_ref[layers:layers + 1].astype(F32)
            for s in range(samples):

                def skip(c, _):
                    both_halves = jnp.concatenate([map_in[s, c + 1, part] for part in range(halves)], axis=1)
                    short[s, c] = jnp.dot(both_halves, w_short[...], preferred_element_type=F32) + skip_bias
                    return 0

                lax.fori_loop(0, cols, skip, 0)
    for s in range(samples):
        activate(layers, s)
        head = lax.dot_general(w_head[...], z_mid[...], (((1,), (1,)), ((), ())), preferred_element_type=F32)
        for ch in range(3):
            out_ref[s, ch] = head[ch * cols:(ch + 1) * cols]

    for k in range(layers + 1):
        for s in range(samples):
            pltpu.make_async_copy(received(k, s), received(k, s), stat_send.at[k, s]).wait()
            for at, there in enumerate((has["left"], has["right"])):
                pl.when(there)(lambda at=at: col_copy(k, s, at).wait_send())
            for at, move in enumerate(row_moves):
                pl.when(move[4])(lambda at=at: row_copy(k, s, at).wait_send())


def solution(mesh):
    rows_n = mesh.shape["sy"]
    cols_n = mesh.shape["sx"]
    tile_spec = P("dp", "sy", "sx", None)
    replicated = P()

    def local_decode(act_in, norm_first, w_first, w_short, norm_rest, w_rest, bias_rest, w_out, bias_out):
        samples, rows, cols, in_ch = act_in.shape
        halves = in_ch // LANES
        layers = w_rest.shape[0] + 1
        peers_n = rows_n * cols_n - 1
        anywhere = pl.BlockSpec(memory_space=pl.ANY)
        in_vmem = pl.BlockSpec(memory_space=pltpu.VMEM)
        image = pl.pallas_call(
            functools.partial(decode_kernel, rows_n, cols_n),
            out_shape=jax.ShapeDtypeStruct((samples, 3, cols, rows), F32),
            in_specs=[anywhere] * 4 + [in_vmem] * 4,
            out_specs=in_vmem,
            scratch_shapes=[
                pltpu.VMEM((samples, rows, cols, in_ch), BF16),
                pltpu.VMEM((samples, halves, rows * cols, LANES), F32),
                pltpu.VMEM((samples, cols + 2, halves, rows, LANES), BF16),
                pltpu.VMEM((layers, samples, cols + 2, rows, LANES), BF16),
                pltpu.VMEM((halves, cols + 2, rows + 16, LANES), F32),
                pltpu.VMEM((rows, (cols + 2) * 3 * in_ch), BF16),
                pltpu.VMEM((rows, (cols + 2) * 3 * LANES), BF16),
                pltpu.VMEM((samples, cols, rows, LANES), F32),
                pltpu.VMEM((4, 3, in_ch, 2 * LANES), BF16),
                pltpu.VMEM((in_ch, LANES), BF16),
                pltpu.VMEM((layers - 1, 4, 3, LANES, 2 * LANES), BF16),
                pltpu.VMEM((4 * cols, (cols + 2) * 3 * LANES), BF16),
                pltpu.VMEM((LANES, LANES), F32),
                pltpu.VMEM((LANES, LANES), F32),
                pltpu.VMEM((samples, 2 * halves, LANES), F32),
                pltpu.VMEM((layers, samples, 2, LANES), F32),
                pltpu.VMEM((samples, peers_n, 2 * halves, LANES), F32),
                pltpu.VMEM((layers, samples, peers_n, 2, LANES), F32),
                pltpu.VMEM((samples, 2, halves, cols, LANES), F32),
                pltpu.VMEM((layers, samples, 2, 1, cols, LANES), F32),
                pltpu.VMEM((samples, 2, 3, halves, cols, LANES), F32),
                pltpu.VMEM((layers, samples, 2, 3, 1, cols, LANES), F32),
                pltpu.SemaphoreType.DMA((samples,)),
                pltpu.SemaphoreType.DMA((layers + 1,)),
                pltpu.SemaphoreType.DMA((layers + 1, samples)),
                pltpu.SemaphoreType.DMA((layers + 1, samples)),
                pltpu.SemaphoreType.DMA((layers + 1, samples, 8)),
                pltpu.SemaphoreType.DMA((layers + 1, samples, 8)),
            ],
            compiler_params=pltpu.CompilerParams(collective_id=0, has_side_effects=True, vmem_limit_bytes=60 * 1024 * 1024),
            name="decode",
        )(act_in, w_first, w_short, w_rest, norm_first, norm_rest, bias_rest, jnp.transpose(w_out, (0, 1, 3, 2)))
        return jnp.transpose(image, (0, 3, 2, 1)) + bias_out.astype(F32)

    return jax.shard_map(local_decode, mesh=mesh, in_specs=(tile_spec,) + (replicated,) * 8, out_specs=tile_spec, check_vma=False)
```

time: 541 us -> 73.7 us (0.14); the launches traced: 533 us -> 73.5 us
  blocking collectives: 322 us -> 0 us
  Pallas kernels: 0 us -> 71.3 us
  matrix products: 60.6 us -> 0 us
  starting transfers between devices: 55.9 us -> 0 us
  waiting for transfers between devices: 53.6 us -> 0 us
  other arithmetic: 33.4 us -> 2.15 us
  local copies, waits for them, and re-layouts: 5.66 us -> 0 us
    psum x7 -> x0, blocking collectives: 322 us -> none  [group_norm_act(): totals = lax.psum(jnp.stack([sum_one, sum_two], axis=-1), ('sy', 'sx'))]
    pallas_call x0 -> x1, Pallas kernels: none -> 71.3 us  [local_decode(): pl.pallas_call(functools.partial(decode_kernel, rows_n, cols_n), out_shap...]
    conv_general_dilated x7 -> x0, matrix products: 59.9 us -> none  [conv_tile(): lax.conv_general_dilated(add_border(act_map), kernel, (1, 1), ((0, 0), (0...]
    ppermute x28 -> x0, starting transfers between devices: 55.9 us -> none  [the longest x7 15.7 us: add_border(): bottom_row = lax.ppermute(act_map[:, :1], 'sy', to_above)]
    ppermute x28 -> x0, waiting for transfers between devices: 53.6 us -> none  [the longest x7 28.8 us: add_border(): right_col = lax.ppermute(tall[:, :, :1], 'sx', to_left)]
    convert_element_type x10 -> x1, other arithmetic: 23 us -> 0.66 us  [local_decode(): return jnp.transpose(image, (0, 3, 2, 1)) + bias_out.astype(F32)]
    reduce_sum x15 -> x0, other arithmetic: 7.16 us -> none  [the longest x8 6.55 us: group_norm_act(): jnp.sum(act_map, axis=(1, 2), dtype=jnp.float32)]
  transfers between devices with their start and end apart: 28 -> 0, of which waited for: 20 -> 0; matrix products, arithmetic and copies ran while one was open for 0% -> 0% of each run, Pallas kernels for 0% -> 0%
where the time goes in v1:
time: 73.7 us; the launch traced here: 73.5 us
  Pallas kernels  71.3 us (97%)
  other arithmetic  2.15 us (3%)
    pallas_call x1, Pallas kernels, local_decode(): pl.pallas_call(functools.partial(decode_kernel, rows_n, cols_n), out_shap...  71.3 us
    add x1, other arithmetic, local_decode(): return jnp.transpose(image, (0, 3, 2, 1)) + bias_out.astype(F32)  1.49 us

profile of v1, /device:TPU:97, one launch (start us, length us, event | category | flops | bytes accessed | tf_op | source)
XLA Modules:
  0.0 73.5 jit_solution(17497531432876750229)
XLA Ops:
  0.0 0.7 convert_element_type.3
  0.7 71.3 %decode.1 = f32[2,3,8,256]{3,2,1,0:T(8,128)} custom-call(bf16[2,256,8,256]{3,2,1,0:T(8,128)(2,1)} %act_hbm.1, bf16[3,3,256,128]{3,2,1,0:T(8,128)(2,1)} %w_first_hbm.1, bf16[256,128]{1,0:T(8,128)(2,1)} %w_short_hbm.1, bf16[5,3,3,128,128]{4,3,2,1,0:T(8,128)(2,1)} %w_rest_hbm.1, bf16[2,256]{1,0:T(2,128)(2,1)} %norm_first_ref.1, ...), custom_call_target="tpu_custom_call" | custom-call | tf_op jit(solution)/shard_map/decode/pallas_call | solution.py:331
  72.0 1.5 %add_bitcast_fusion = f32[2,256,8,3]{1,2,3,0:T(8,128)} fusion(f32[2,3,8,256]{3,2,1,0:T(8,128)} %decode.1, f32[3]{0:T(128)S(1)} %convert_element_type.3), kind=kLoop, calls=%fused_computation | loop fusion | flops 12288 | bytes 98316 | tf_op jit(solution)/shard_map/add | solution.py:369

commit v2 on v1

v2 whole, which is shorter than its diff:
```python
import functools

import jax
import jax.numpy as jnp
from jax import lax
from jax.experimental import pallas as pl
from jax.experimental.pallas import tpu as pltpu
from jax.sharding import PartitionSpec as P

GROUPS = 32
GN_EPS = 1e-6
LANES = 128
MESH = pl.DeviceIdType.MESH
F32 = jnp.float32
BF16 = jnp.bfloat16


def half_silu(half):
    return half + half * jnp.tanh(half)


def decode_kernel(rows_n, cols_n, act_hbm, w_first_hbm, w_short_hbm, w_rest_hbm, norm_first_hbm, norm_rest_hbm, bias_hbm, w_out_hbm, bias_out_ref, out_ref,
                  raw, flat, map_in, maps, z_in, z_mid, short, w_first, w_short, w_rest, w_head, ones_in, ones_mid,
                  norm_first_ref, norm_rest_ref, bias_ref, bias_rows, w_out_ref,
                  msg_in, msg_mid, got_in, got_mid, edge_in, edge_mid, halo_in, halo_mid, halo_act,
                  act_sem, weight_sem, small_sem, stat_recv, stat_send, halo_recv, halo_send):
    samples, rows, cols, in_ch = raw.shape
    halves = in_ch // LANES
    layers = w_rest.shape[0] + 1
    peers_n = rows_n * cols_n - 1
    sx = lax.axis_index("sx")
    sy = lax.axis_index("sy")
    core = lax.rem(sy, 2)
    chip = sy // 2
    chips_n = rows_n // 2

    def ring(offset, size):
        return min(offset, size - offset)

    offsets = [(dx, dy, dc) for dx in range(cols_n) for dy in range(chips_n) for dc in range(2) if (dx, dy, dc) != (0, 0, 0)]
    offsets.sort(key=lambda o: (-ring(o[0], cols_n) - ring(o[1], chips_n), o[2]))

    def peer(offset):
        dx, dy, dc = offset
        return {"sx": lax.rem(sx + dx, cols_n), "sy": lax.rem(chip + dy, chips_n) * 2 + (1 - core if dc else core)}

    barrier = pltpu.get_barrier_semaphore()
    for offset in offsets:
        pl.semaphore_signal(barrier, inc=1, device_id=peer(offset), device_id_type=MESH)

    for s in range(samples):
        pltpu.make_async_copy(act_hbm.at[s], raw.at[s], act_sem.at[s]).start()
    small = [(norm_first_hbm, norm_first_ref), (norm_rest_hbm, norm_rest_ref), (bias_hbm, bias_ref), (w_out_hbm, w_out_ref)]
    for at, (src, dst) in enumerate(small):
        pltpu.make_async_copy(src, dst, small_sem.at[at]).start()
    pltpu.make_async_copy(w_short_hbm, w_short, weight_sem.at[layers]).start()
    for o in range(2):
        for dc in range(3):
            pltpu.make_async_copy(w_first_hbm.at[:, dc], w_first.at[o + dc, :, :, pl.ds(o * LANES, LANES)], weight_sem.at[0]).start()

    has = {"up": sy > 0, "down": sy < rows_n - 1, "left": sx > 0, "right": sx < cols_n - 1}

    def both(one, two):
        return jnp.logical_and(has[one], has[two])

    row_moves = [
        (1, 1, 0, {"sy": sy - 1}, has["up"], has["down"]),
        (0, 1, 1, {"sy": sy + 1}, has["down"], has["up"]),
        (1, 2, 0, {"sx": sx - 1, "sy": sy - 1}, both("up", "left"), both("down", "right")),
        (1, 0, 0, {"sx": sx + 1, "sy": sy - 1}, both("up", "right"), both("down", "left")),
        (0, 2, 1, {"sx": sx - 1, "sy": sy + 1}, both("down", "left"), both("up", "right")),
        (0, 0, 1, {"sx": sx + 1, "sy": sy + 1}, both("down", "right"), both("up", "left")),
    ]

    def is_first(k):
        return isinstance(k, int) and k == 0

    def tile(k, s, c):
        return map_in.at[s, c] if is_first(k) else maps.at[k - 1, s, c]

    def edges(k, s):
        return edge_in.at[s] if is_first(k) else edge_mid.at[k - 1, s]

    def halo(k, s):
        return halo_in.at[s] if is_first(k) else halo_mid.at[k - 1, s]

    def message(k, s):
        return msg_in if is_first(k) else msg_mid.at[k - 1, s]

    def received(k, s):
        return got_in if is_first(k) else got_mid.at[k - 1, s]

    def col_copy(k, s, at):
        src, dst, to = ((1, cols + 1, {"sx": sx - 1}), (cols, 0, {"sx": sx + 1}))[at]
        return pltpu.make_async_remote_copy(tile(k, s, src), tile(k, s, dst), halo_send.at[k, s, at], halo_recv.at[k, s, at], device_id=to, device_id_type=MESH)

    def row_copy(k, s, at):
        side, place, edge, to, _, _ = row_moves[at]
        return pltpu.make_async_remote_copy(edges(k, s).at[edge], halo(k, s).at[side, place], halo_send.at[k, s, 2 + at], halo_recv.at[k, s, 2 + at], device_id=to, device_id_type=MESH)

    def send_cols(k, s):
        for at, there in enumerate((has["left"], has["right"])):
            pl.when(there)(lambda at=at: col_copy(k, s, at).start())

    def send_rows(k, s):
        for at, move in enumerate(row_moves):
            pl.when(move[4])(lambda at=at: row_copy(k, s, at).start())

    def send_stats(k, s):
        for slot, offset in enumerate(offsets):
            pltpu.make_async_remote_copy(message(k, s), received(k, s).at[slot], stat_send.at[k, s], stat_recv.at[k, s], device_id=peer(offset), device_id_type=MESH).start()

    def sent(k, s, first=None):
        if first is None:
            pltpu.make_async_copy(received(k, s), received(k, s), stat_send.at[k, s]).wait()
        for at, there in enumerate((has["left"], has["right"])):
            pl.when(there)(lambda at=at: col_copy(k, s, at).wait_send())
        for at, move in enumerate(row_moves):
            pl.when(move[4])(lambda at=at: row_copy(k, s, at).wait_send())

    def scales(k, s):
        if is_first(k):
            total = msg_in[s] + jnp.sum(got_in[:, s], axis=0)
        else:
            pltpu.make_async_copy(received(k, s), received(k, s), stat_recv.at[k, s]).wait()
            total = message(k, s)[...] + jnp.sum(received(k, s)[...], axis=0)
        ones = ones_in if is_first(k) else ones_mid
        total = jnp.dot(total, ones[...], precision=lax.Precision.HIGHEST, preferred_element_type=F32)
        parts = halves if is_first(k) else 1
        per_group = parts * LANES // GROUPS
        count = rows * rows_n * cols * cols_n * per_group
        rows_out = []
        for part in range(parts):
            norm = (norm_first_ref[:, part * LANES:(part + 1) * LANES] if is_first(k) else norm_rest_ref[k - 1]).astype(F32)
            mean = total[part:part + 1] / count
            square = total[parts + part:parts + part + 1] / count
            scale = lax.rsqrt(square - mean * mean + GN_EPS) * norm[0:1]
            shift = norm[1:2] - mean * scale
            rows_out.append((0.5 * scale, 0.5 * shift))
        return rows_out

    def activate_rows(k, s, scale_rows):
        for at, move in enumerate(row_moves):
            pl.when(move[5])(lambda at=at: row_copy(k, s, at).wait_recv())
        for part, (scale, shift) in enumerate(scale_rows):
            for side, there in ((0, "up"), (1, "down")):
                for place in range(3):
                    seen = has[there] if place == 1 else both(there, "left" if place == 0 else "right")
                    act = half_silu(halo(k, s)[side, place, part] * scale + shift)
                    halo_act[side, part, place * cols:(place + 1) * cols, :] = jnp.where(seen, act, 0.0)

    def activate(k, s, scale_rows, c):
        z = z_in if is_first(k) else z_mid
        parts = len(scale_rows)
        for part, (scale, shift) in enumerate(scale_rows):
            ref = map_in.at[s, c, part] if is_first(k) else maps.at[k - 1, s, c]
            act = half_silu(ref[...].astype(F32) * scale + shift)
            if c in (0, cols + 1):
                act = jnp.where(has["left" if c == 0 else "right"], act, 0.0)
            at = cols - 1 + c
            above = jnp.concatenate([halo_act[0, part, at:at + 1, :], act[:-1]], axis=0)
            below = jnp.concatenate([act[1:], halo_act[1, part, at:at + 1, :]], axis=0)
            for dr, value in enumerate((above, act, below)):
                z[(c * 3 + dr) * parts + part] = value.astype(BF16)

    def wait_cols(k, s):
        for at, there in enumerate((has["right"], has["left"])):
            pl.when(there)(lambda at=at: col_copy(k, s, at).wait_recv())

    def layer(k, s, skip):
        z = z_in if is_first(k) else z_mid
        scale_rows = scales(k, s)
        parts = len(scale_rows)
        depth = 3 * parts
        weights = (w_first[...] if is_first(k) else w_rest[k - 1]).reshape(4 * depth * LANES, 2 * LANES)
        bias = bias_rows[k]
        edge = edges(k + 1, s)

        def pair(p, sums):
            lhs = jnp.concatenate([z[2 * p * depth + i] for i in range(4 * depth)], axis=1)
            acc = jnp.dot(lhs, weights, preferred_element_type=F32)
            sum_one, sum_two = sums
            for o in range(2):
                c = 2 * p + o
                value = acc[:, o * LANES:(o + 1) * LANES] + bias
                if skip == "input":
                    value = value + short[s, c]
                elif skip == "map":
                    value = value + maps[k - 2, s, c + 1].astype(F32)
                rounded = value.astype(BF16)
                maps[k, s, c + 1] = rounded
                value = rounded.astype(F32)
                edge[0, 0, c:c + 1, :] = value[0:1]
                edge[1, 0, c:c + 1, :] = value[rows - 1:rows]
                value = value.reshape(rows // 8, 8, LANES)
                sum_one = sum_one + jnp.sum(value, axis=0)
                sum_two = sum_two + jnp.sum(value * value, axis=0)
            return sum_one, sum_two

        zero = jnp.zeros((8, LANES), F32)
        sums = (zero, zero)
        activate_rows(k, s, scale_rows)
        done = set()
        order = list(range(1, cols // 2 - 1)) + [0, cols // 2 - 1]
        for p in order:
            if p == 0:
                for c in range(1, cols + 1):
                    if c not in done:
                        activate(k, s, scale_rows, c)
                        done.add(c)
                wait_cols(k, s)
            for c in range(2 * p, 2 * p + 4):
                if c not in done:
                    activate(k, s, scale_rows, c)
                    done.add(c)
            sums = pair(p, sums)
        target = message(k + 1, s)
        for at, part in enumerate(sums):
            target[at:at + 1, :] = jnp.sum(part, axis=0, keepdims=True)
        send_stats(k + 1, s)
        send_rows(k + 1, s)
        send_cols(k + 1, s)
        sent(k, s, first=True if is_first(k) else None)

    chunk = 16

    def load(s):
        pltpu.make_async_copy(act_hbm.at[s], raw.at[s], act_sem.at[s]).wait()

        def step(i, sums):
            at = pl.multiple_of(i * chunk, chunk)
            sums = list(sums)
            for part in range(halves):
                value = raw[s, pl.ds(at, chunk), :, part * LANES:(part + 1) * LANES].astype(F32)
                flat[s, part, pl.ds(pl.multiple_of(at * cols, chunk * cols), chunk * cols), :] = value.reshape(chunk * cols, LANES)
                sums[part] = sums[part] + jnp.sum(value, axis=0)
                sums[halves + part] = sums[halves + part] + jnp.sum(value * value, axis=0)
            return tuple(sums)

        zero = jnp.zeros((cols, LANES), F32)
        sums = lax.fori_loop(0, rows // chunk, step, (zero,) * (2 * halves))
        for at, part in enumerate(sums):
            msg_in[s, at:at + 1, :] = jnp.sum(part, axis=0, keepdims=True)
        for part in range(halves):
            edge_in[s, 0, part] = flat[s, part, 0:cols, :]
            edge_in[s, 1, part] = flat[s, part, (rows - 1) * cols:, :]

    def turn(s, c):
        for part in range(halves):
            map_in[s, c + 1, part] = flat[s, part, pl.ds(c, rows, stride=cols), :].astype(BF16)

    for s in range(samples):
        load(s)
    pl.semaphore_wait(barrier, peers_n)
    send_stats(0, 0)
    for s in range(samples):
        turn(s, 0)
        turn(s, cols - 1)
        send_rows(0, s)
        send_cols(0, s)

    for k in range(layers - 1):
        for o in range(2):
            for dc in range(3):
                pltpu.make_async_copy(w_rest_hbm.at[k, :, dc], w_rest.at[k, o + dc, :, :, pl.ds(o * LANES, LANES)], weight_sem.at[k + 1]).start()
    for src_dst, at in zip(small, range(len(small))):
        pltpu.make_async_copy(*src_dst, small_sem.at[at]).wait()
    row_id = lax.broadcasted_iota(jnp.int32, (LANES, LANES), 0)
    lane_id = lax.broadcasted_iota(jnp.int32, (LANES, LANES), 1)
    for ones, per_group in ((ones_in, in_ch // GROUPS), (ones_mid, LANES // GROUPS)):
        ones[...] = jnp.where(row_id // per_group == lane_id // per_group, 1.0, 0.0).astype(F32)
    for dr in range(3):
        w_first[3, dr, :, 0:LANES] = jnp.zeros((in_ch, LANES), BF16)
        w_first[0, dr, :, LANES:] = jnp.zeros((in_ch, LANES), BF16)
    pltpu.make_async_copy(w_short_hbm, w_short, weight_sem.at[layers]).wait()
    for at in range(layers + 1):
        bias_rows[at] = bias_ref[at:at + 1].astype(F32)
    skip_bias = bias_rows[layers]
    def skip_product(s, _):
        for c in range(cols):
            if 0 < c < cols - 1:
                turn(s, c)
            both_halves = jnp.concatenate([map_in[s, c + 1, part] for part in range(halves)], axis=1)
            short[s, c] = jnp.dot(both_halves, w_short[...], preferred_element_type=F32) + skip_bias
        return 0

    lax.fori_loop(0, samples, skip_product, 0)

    def clear(k, _):
        for dr in range(3):
            w_rest[k, 3, dr, :, 0:LANES] = jnp.zeros((LANES, LANES), BF16)
            w_rest[k, 0, dr, :, LANES:] = jnp.zeros((LANES, LANES), BF16)
        return 0

    lax.fori_loop(0, layers - 1, clear, 0)

    col_id = lax.broadcasted_iota(jnp.int32, (cols, LANES), 0)

    def head_block(j, _):
        for dr in range(3):
            blocks = []
            for ch in range(3):
                block = jnp.zeros((cols, LANES), F32)
                for dc in range(3):
                    block = jnp.where(col_id == j - dc, w_out_ref[dr, dc, ch:ch + 1, :].astype(F32), block)
                blocks.append(block)
            blocks.append(jnp.zeros((cols, LANES), F32))
            w_head[:, pl.ds(pl.multiple_of((j * 3 + dr) * LANES, LANES), LANES)] = jnp.concatenate(blocks, axis=0).astype(BF16)
        return 0

    lax.fori_loop(0, cols + 2, head_block, 0)

    def both_samples(k, skip):
        lax.fori_loop(0, samples, lambda s, _: (layer(k, s, skip), 0)[1], 0)

    def weights_here(k):
        pltpu.make_async_copy(w_rest.at[k - 1, 0:3], w_rest.at[k - 1, 0:3], weight_sem.at[k]).wait()

    pltpu.make_async_copy(w_first.at[0:3], w_first.at[0:3], weight_sem.at[0]).wait()
    pltpu.make_async_copy(got_in, got_in, stat_recv.at[0, 0]).wait()
    both_samples(0, None)
    pltpu.make_async_copy(got_in, got_in, stat_send.at[0, 0]).wait()
    weights_here(1)
    both_samples(1, "input")

    def block(i, _):
        weights_here(2 * i)
        both_samples(2 * i, None)
        weights_here(2 * i + 1)
        both_samples(2 * i + 1, "map")
        return 0

    lax.fori_loop(1, layers // 2, block, 0)

    def head(s, _):
        scale_rows = scales(layers, s)
        activate_rows(layers, s, scale_rows)
        for c in range(1, cols + 1):
            activate(layers, s, scale_rows, c)
        wait_cols(layers, s)
        activate(layers, s, scale_rows, 0)
        activate(layers, s, scale_rows, cols + 1)
        acts = jnp.concatenate([z_mid[i] for i in range(3 * (cols + 2))], axis=1)
        rgb = lax.dot_general(w_head[...], acts, (((1,), (1,)), ((), ())), preferred_element_type=F32)
        for ch in range(3):
            out_ref[s, ch] = rgb[ch * cols:(ch + 1) * cols] + bias_out_ref[:, ch:ch + 1].astype(F32)
        sent(layers, s)
        return 0

    lax.fori_loop(0, samples, head, 0)


def solution(mesh):
    rows_n = mesh.shape["sy"]
    cols_n = mesh.shape["sx"]
    tile_spec = P("dp", "sy", "sx", None)
    replicated = P()

    def local_decode(act_in, norm_first, w_first, w_short, norm_rest, w_rest, bias_rest, w_out, bias_out):
        samples, rows, cols, in_ch = act_in.shape
        halves = in_ch // LANES
        layers = w_rest.shape[0] + 1
        peers_n = rows_n * cols_n - 1
        anywhere = pl.BlockSpec(memory_space=pl.ANY)
        in_vmem = pl.BlockSpec(memory_space=pltpu.VMEM)
        image = pl.pallas_call(
            functools.partial(decode_kernel, rows_n, cols_n),
            out_shape=jax.ShapeDtypeStruct((samples, 3, cols, rows), F32),
            in_specs=[anywhere] * 8 + [in_vmem],
            out_specs=in_vmem,
            scratch_shapes=[
                pltpu.VMEM((samples, rows, cols, in_ch), BF16),
                pltpu.VMEM((samples, halves, rows * cols, LANES), F32),
                pltpu.VMEM((samples, cols + 2, halves, rows, LANES), BF16),
                pltpu.VMEM((layers, samples, cols + 2, rows, LANES), BF16),
                pltpu.VMEM(((cols + 2) * 3 * halves, rows, LANES), BF16),
                pltpu.VMEM(((cols + 2) * 3, rows, LANES), BF16),
                pltpu.VMEM((samples, cols, rows, LANES), F32),
                pltpu.VMEM((4, 3, in_ch, 2 * LANES), BF16),
                pltpu.VMEM((in_ch, LANES), BF16),
                pltpu.VMEM((layers - 1, 4, 3, LANES, 2 * LANES), BF16),
                pltpu.VMEM((4 * cols, (cols + 2) * 3 * LANES), BF16),
                pltpu.VMEM((LANES, LANES), F32),
                pltpu.VMEM((LANES, LANES), F32),
                pltpu.VMEM(norm_first.shape, BF16),
                pltpu.VMEM(norm_rest.shape, BF16),
                pltpu.VMEM(bias_rest.shape, BF16),
                pltpu.VMEM((bias_rest.shape[0], 1, LANES), F32),
                pltpu.VMEM((3, 3, 3, LANES), BF16),
                pltpu.VMEM((samples, 2 * halves, LANES), F32),
                pltpu.VMEM((layers, samples, 2, LANES), F32),
                pltpu.VMEM((peers_n, samples, 2 * halves, LANES), F32),
                pltpu.VMEM((layers, samples, peers_n, 2, LANES), F32),
                pltpu.VMEM((samples, 2, halves, cols, LANES), F32),
                pltpu.VMEM((layers, samples, 2, 1, cols, LANES), F32),
                pltpu.VMEM((samples, 2, 3, halves, cols, LANES), F32),
                pltpu.VMEM((layers, samples, 2, 3, 1, cols, LANES), F32),
                pltpu.VMEM((2, halves, 3 * cols, LANES), F32),
                pltpu.SemaphoreType.DMA((samples,)),
                pltpu.SemaphoreType.DMA((layers + 1,)),
                pltpu.SemaphoreType.DMA((4,)),
                pltpu.SemaphoreType.DMA((layers + 1, samples)),
                pltpu.SemaphoreType.DMA((layers + 1, samples)),
                pltpu.SemaphoreType.DMA((layers + 1, samples, 8)),
                pltpu.SemaphoreType.DMA((layers + 1, samples, 8)),
            ],
            compiler_params=pltpu.CompilerParams(collective_id=0, has_side_effects=True, vmem_limit_bytes=60 * 1024 * 1024),
            name="decode",
        )(act_in, w_first, w_short, w_rest, norm_first, norm_rest, bias_rest, jnp.transpose(w_out, (0, 1, 3, 2)), bias_out.reshape(1, 3))
        return jnp.transpose(image, (0, 3, 2, 1))

    return jax.shard_map(local_decode, mesh=mesh, in_specs=(tile_spec,) + (replicated,) * 8, out_specs=tile_spec, check_vma=False)
```

time: 73.7 us -> 63.9 us (0.87)
  Pallas kernels: 71.3 us -> 62.3 us
  other arithmetic: 2.15 us -> 0 us
  local copies, waits for them, and re-layouts: 0 us -> 1.42 us
    pallas_call x1, Pallas kernels: 71.3 us -> 62.3 us  [local_decode(): pl.pallas_call(functools.partial(decode_kernel, rows_n, cols_n), out_shap...]
    add x1 -> x0, other arithmetic: 1.49 us -> none  [local_decode(): return jnp.transpose(image, (0, 3, 2, 1)) + bias_out.astype(F32)]
    unnamed x0 -> x1, local copies, waits for them, and re-layouts: none -> 1.42 us
where the time goes in v2:
time: 63.9 us; the launch traced here: 63.7 us
  Pallas kernels  62.3 us (97%)
  local copies, waits for them, and re-layouts  1.42 us (2%)
    pallas_call x1, Pallas kernels, local_decode(): pl.pallas_call(functools.partial(decode_kernel, rows_n, cols_n), out_shap...  62.3 us
    unnamed x1, local copies, waits for them, and re-layouts  1.42 us

profile of v2, /device:TPU:97, one launch (start us, length us, event | category | flops | bytes accessed | tf_op | source)
XLA Modules:
  0.0 63.7 jit_solution(9370742289246057142)
XLA Ops:
  0.0 62.3 %decode.1 = f32[2,3,8,256]{3,2,1,0:T(8,128)} custom-call(bf16[2,256,8,256]{3,2,1,0:T(8,128)(2,1)} %act_hbm.1, bf16[3,3,256,128]{3,2,1,0:T(8,128)(2,1)} %w_first_hbm.1, bf16[256,128]{1,0:T(8,128)(2,1)} %w_short_hbm.1, bf16[5,3,3,128,128]{4,3,2,1,0:T(8,128)(2,1)} %w_rest_hbm.1, bf16[2,256]{1,0:T(2,128)(2,1)} %norm_first_hbm.1, ...), custom_call_target="tpu_custom_call" | custom-call | tf_op jit(solution)/shard_map/decode/pallas_call | solution.py:366
  62.3 1.4 %copy.11 = f32[2,256,8,3]{1,2,3,0:T(8,128)} copy(f32[2,256,8,3]{1,2,3,0:T(8,128)} %bitcast.3) | data formatting | bytes 98304

commit v3 on v2

--- a/solution.py
+++ b/solution.py
@@ -20,7 +20,7 @@
 
 
 def decode_kernel(rows_n, cols_n, act_hbm, w_first_hbm, w_short_hbm, w_rest_hbm, norm_first_hbm, norm_rest_hbm, bias_hbm, w_out_hbm, bias_out_ref, out_ref,
-                  raw, flat, map_in, maps, z_in, z_mid, short, w_first, w_short, w_rest, w_head, ones_in, ones_mid,
+                  raw, flat, map_in, mid_maps, hidden_maps, z_in, z_mid, short, w_first, w_short, w_rest, w_head, ones_in, ones_mid,
                   norm_first_ref, norm_rest_ref, bias_ref, bias_rows, w_out_ref,
                   msg_in, msg_mid, got_in, got_mid, edge_in, edge_mid, halo_in, halo_mid, halo_act,
                   act_sem, weight_sem, small_sem, stat_recv, stat_send, halo_recv, halo_send):
@@ -73,30 +73,38 @@
     ]
 
     def is_first(k):
-        return isinstance(k, int) and k == 0
+        return k[1] == 0 and isinstance(k[0], int) and k[0] == 0
+
+    def number(k):
+        return 2 * k[0] + k[1]
+
+    def following(k):
+        return (k[0], 1) if k[1] == 0 else (k[0] + 1, 0)
 
     def tile(k, s, c):
-        return map_in.at[s, c] if is_first(k) else maps.at[k - 1, s, c]
+        if is_first(k):
+            return map_in.at[s, c]
+        return mid_maps.at[k[0], s, c] if k[1] else hidden_maps.at[k[0] - 1, s, c]
 
     def edges(k, s):
-        return edge_in.at[s] if is_first(k) else edge_mid.at[k - 1, s]
+        return edge_in.at[s] if is_first(k) else edge_mid.at[number(k) - 1, s]
 
     def halo(k, s):
-        return halo_in.at[s] if is_first(k) else halo_mid.at[k - 1, s]
+        return halo_in.at[s] if is_first(k) else halo_mid.at[number(k) - 1, s]
 
     def message(k, s):
-        return msg_in if is_first(k) else msg_mid.at[k - 1, s]
+        return msg_in if is_first(k) else msg_mid.at[number(k) - 1, s]
 
     def received(k, s):
-        return got_in if is_first(k) else got_mid.at[k - 1, s]
+        return got_in if is_first(k) else got_mid.at[number(k) - 1, s]
 
     def col_copy(k, s, at):
         src, dst, to = ((1, cols + 1, {"sx": sx - 1}), (cols, 0, {"sx": sx + 1}))[at]
-        return pltpu.make_async_remote_copy(tile(k, s, src), tile(k, s, dst), halo_send.at[k, s, at], halo_recv.at[k, s, at], device_id=to, device_id_type=MESH)
+        return pltpu.make_async_remote_copy(tile(k, s, src), tile(k, s, dst), halo_send.at[number(k), s, at], halo_recv.at[number(k), s, at], device_id=to, device_id_type=MESH)
 
     def row_copy(k, s, at):
         side, place, edge, to, _, _ = row_moves[at]
-        return pltpu.make_async_remote_copy(edges(k, s).at[edge], halo(k, s).at[side, place], halo_send.at[k, s, 2 + at], halo_recv.at[k, s, 2 + at], device_id=to, device_id_type=MESH)
+        return pltpu.make_async_remote_copy(edges(k, s).at[edge], halo(k, s).at[side, place], halo_send.at[number(k), s, 2 + at], halo_recv.at[number(k), s, 2 + at], device_id=to, device_id_type=MESH)
 
     def send_cols(k, s):
         for at, there in enumerate((has["left"], has["right"])):
@@ -108,11 +116,11 @@
 
     def send_stats(k, s):
         for slot, offset in enumerate(offsets):
-            pltpu.make_async_remote_copy(message(k, s), received(k, s).at[slot], stat_send.at[k, s], stat_recv.at[k, s], device_id=peer(offset), device_id_type=MESH).start()
+            pltpu.make_async_remote_copy(message(k, s), received(k, s).at[slot], stat_send.at[number(k), s], stat_recv.at[number(k), s], device_id=peer(offset), device_id_type=MESH).start()
 
     def sent(k, s, first=None):
         if first is None:
-            pltpu.make_async_copy(received(k, s), received(k, s), stat_send.at[k, s]).wait()
+            pltpu.make_async_copy(received(k, s), received(k, s), stat_send.at[number(k), s]).wait()
         for at, there in enumerate((has["left"], has["right"])):
             pl.when(there)(lambda at=at: col_copy(k, s, at).wait_send())
         for at, move in enumerate(row_moves):
@@ -122,16 +130,20 @@
         if is_first(k):
             total = msg_in[s] + jnp.sum(got_in[:, s], axis=0)
         else:
-            pltpu.make_async_copy(received(k, s), received(k, s), stat_recv.at[k, s]).wait()
+            pltpu.make_async_copy(received(k, s), received(k, s), stat_recv.at[number(k), s]).wait()
             total = message(k, s)[...] + jnp.sum(received(k, s)[...], axis=0)
         ones = ones_in if is_first(k) else ones_mid
-        total = jnp.dot(total, ones[...], precision=lax.Precision.HIGHEST, preferred_element_type=F32)
+        high = total.astype(BF16)
+        rest = total - high.astype(F32)
+        middle = rest.astype(BF16)
+        low = (rest - middle.astype(F32)).astype(BF16)
+        total = sum(jnp.dot(piece, ones[...], preferred_element_type=F32) for piece in (low, middle, high))
         parts = halves if is_first(k) else 1
         per_group = parts * LANES // GROUPS
         count = rows * rows_n * cols * cols_n * per_group
         rows_out = []
         for part in range(parts):
-            norm = (norm_first_ref[:, part * LANES:(part + 1) * LANES] if is_first(k) else norm_rest_ref[k - 1]).astype(F32)
+            norm = (norm_first_ref[:, part * LANES:(part + 1) * LANES] if is_first(k) else norm_rest_ref[number(k) - 1]).astype(F32)
             mean = total[part:part + 1] / count
             square = total[parts + part:parts + part + 1] / count
             scale = lax.rsqrt(square - mean * mean + GN_EPS) * norm[0:1]
@@ -153,7 +165,7 @@
         z = z_in if is_first(k) else z_mid
         parts = len(scale_rows)
         for part, (scale, shift) in enumerate(scale_rows):
-            ref = map_in.at[s, c, part] if is_first(k) else maps.at[k - 1, s, c]
+            ref = tile(k, s, c).at[part] if is_first(k) else tile(k, s, c)
             act = half_silu(ref[...].astype(F32) * scale + shift)
             if c in (0, cols + 1):
                 act = jnp.where(has["left" if c == 0 else "right"], act, 0.0)
@@ -167,14 +179,15 @@
         for at, there in enumerate((has["right"], has["left"])):
             pl.when(there)(lambda at=at: col_copy(k, s, at).wait_recv())
 
-    def layer(k, s, skip):
+    def layer(k, s):
         z = z_in if is_first(k) else z_mid
         scale_rows = scales(k, s)
         parts = len(scale_rows)
         depth = 3 * parts
-        weights = (w_first[...] if is_first(k) else w_rest[k - 1]).reshape(4 * depth * LANES, 2 * LANES)
-        bias = bias_rows[k]
-        edge = edges(k + 1, s)
+        weights = (w_first[...] if is_first(k) else w_rest[number(k) - 1]).reshape(4 * depth * LANES, 2 * LANES)
+        bias = bias_rows[number(k)]
+        later = following(k)
+        edge = edges(later, s)
 
         def pair(p, sums):
             lhs = jnp.concatenate([z[2 * p * depth + i] for i in range(4 * depth)], axis=1)
@@ -183,13 +196,13 @@
             for o in range(2):
                 c = 2 * p + o
                 value = acc[:, o * LANES:(o + 1) * LANES] + bias
-                if skip == "input":
+                if k[1]:
                     value = value + short[s, c]
-                elif skip == "map":
-                    value = value + maps[k - 2, s, c + 1].astype(F32)
                 rounded = value.astype(BF16)
-                maps[k, s, c + 1] = rounded
+                tile(later, s, c + 1)[...] = rounded
                 value = rounded.astype(F32)
+                if k[1]:
+                    short[s, c] = value
                 edge[0, 0, c:c + 1, :] = value[0:1]
                 edge[1, 0, c:c + 1, :] = value[rows - 1:rows]
                 value = value.reshape(rows // 8, 8, LANES)
@@ -214,12 +227,12 @@
                     activate(k, s, scale_rows, c)
                     done.add(c)
             sums = pair(p, sums)
-        target = message(k + 1, s)
+        target = message(later, s)
         for at, part in enumerate(sums):
             target[at:at + 1, :] = jnp.sum(part, axis=0, keepdims=True)
-        send_stats(k + 1, s)
-        send_rows(k + 1, s)
-        send_cols(k + 1, s)
+        send_stats(later, s)
+        send_rows(later, s)
+        send_cols(later, s)
         sent(k, s, first=True if is_first(k) else None)
 
     chunk = 16
@@ -249,15 +262,17 @@
         for part in range(halves):
             map_in[s, c + 1, part] = flat[s, part, pl.ds(c, rows, stride=cols), :].astype(BF16)
 
+    first = (0, 0)
     for s in range(samples):
         load(s)
-    pl.semaphore_wait(barrier, peers_n)
-    send_stats(0, 0)
     for s in range(samples):
         turn(s, 0)
         turn(s, cols - 1)
-        send_rows(0, s)
-        send_cols(0, s)
+    pl.semaphore_wait(barrier, peers_n)
+    send_stats(first, 0)
+    for s in range(samples):
+        send_rows(first, s)
+        send_cols(first, s)
 
     for k in range(layers - 1):
         for o in range(2):
@@ -268,7 +283,7 @@
     row_id = lax.broadcasted_iota(jnp.int32, (LANES, LANES), 0)
     lane_id = lax.broadcasted_iota(jnp.int32, (LANES, LANES), 1)
     for ones, per_group in ((ones_in, in_ch // GROUPS), (ones_mid, LANES // GROUPS)):
-        ones[...] = jnp.where(row_id // per_group == lane_id // per_group, 1.0, 0.0).astype(F32)
+        ones[...] = jnp.where(row_id // per_group == lane_id // per_group, 1.0, 0.0).astype(BF16)
     for dr in range(3):
         w_first[3, dr, :, 0:LANES] = jnp.zeros((in_ch, LANES), BF16)
         w_first[0, dr, :, LANES:] = jnp.zeros((in_ch, LANES), BF16)
@@ -310,41 +325,45 @@
 
     lax.fori_loop(0, cols + 2, head_block, 0)
 
-    def both_samples(k, skip):
-        lax.fori_loop(0, samples, lambda s, _: (layer(k, s, skip), 0)[1], 0)
-
-    def weights_here(k):
-        pltpu.make_async_copy(w_rest.at[k - 1, 0:3], w_rest.at[k - 1, 0:3], weight_sem.at[k]).wait()
+    def both_samples(k):
+        if not is_first(k):
+            at = number(k) - 1
+            pltpu.make_async_copy(w_rest.at[at, 0:3], w_rest.at[at, 0:3], weight_sem.at[at + 1]).wait()
+        lax.fori_loop(0, samples, lambda s, _: (layer(k, s), 0)[1], 0)
 
     pltpu.make_async_copy(w_first.at[0:3], w_first.at[0:3], weight_sem.at[0]).wait()
     pltpu.make_async_copy(got_in, got_in, stat_recv.at[0, 0]).wait()
-    both_samples(0, None)
+    both_samples(first)
     pltpu.make_async_copy(got_in, got_in, stat_send.at[0, 0]).wait()
-    weights_here(1)
-    both_samples(1, "input")
+    both_samples((0, 1))
 
     def block(i, _):
-        weights_here(2 * i)
-        both_samples(2 * i, None)
-        weights_here(2 * i + 1)
-        both_samples(2 * i + 1, "map")
+        both_samples((i, 0))
+        both_samples((i, 1))
         return 0
 
     lax.fori_loop(1, layers // 2, block, 0)
+    last = (layers // 2, 0)
 
     def head(s, _):
-        scale_rows = scales(layers, s)
-        activate_rows(layers, s, scale_rows)
+        scale_rows = scales(last, s)
+        activate_rows(last, s, scale_rows)
+
+        def product(blocks):
+            acts = jnp.concatenate([z_mid[i] for i in blocks], axis=1)
+            weights = w_head[:, blocks[0] * LANES:(blocks[-1] + 1) * LANES]
+            return lax.dot_general(weights, acts, (((1,), (1,)), ((), ())), preferred_element_type=F32)
+
         for c in range(1, cols + 1):
-            activate(layers, s, scale_rows, c)
-        wait_cols(layers, s)
-        activate(layers, s, scale_rows, 0)
-        activate(layers, s, scale_rows, cols + 1)
-        acts = jnp.concatenate([z_mid[i] for i in range(3 * (cols + 2))], axis=1)
-        rgb = lax.dot_general(w_head[...], acts, (((1,), (1,)), ((), ())), preferred_element_type=F32)
+            activate(last, s, scale_rows, c)
+        rgb = product(range(3, 3 * (cols + 1)))
+        wait_cols(last, s)
+        for c in (0, cols + 1):
+            activate(last, s, scale_rows, c)
+            rgb = rgb + product(range(3 * c, 3 * c + 3))
         for ch in range(3):
             out_ref[s, ch] = rgb[ch * cols:(ch + 1) * cols] + bias_out_ref[:, ch:ch + 1].astype(F32)
-        sent(layers, s)
+        sent(last, s)
         return 0
 
     lax.fori_loop(0, samples, head, 0)
@@ -372,7 +391,8 @@
                 pltpu.VMEM((samples, rows, cols, in_ch), BF16),
                 pltpu.VMEM((samples, halves, rows * cols, LANES), F32),
                 pltpu.VMEM((samples, cols + 2, halves, rows, LANES), BF16),
-                pltpu.VMEM((layers, samples, cols + 2, rows, LANES), BF16),
+                pltpu.VMEM(((layers + 1) // 2, samples, cols + 2, rows, LANES), BF16),
+                pltpu.VMEM(((layers + 1) // 2, samples, cols + 2, rows, LANES), BF16),
                 pltpu.VMEM(((cols + 2) * 3 * halves, rows, LANES), BF16),
                 pltpu.VMEM(((cols + 2) * 3, rows, LANES), BF16),
                 pltpu.VMEM((samples, cols, rows, LANES), F32),
@@ -380,8 +400,8 @@
                 pltpu.VMEM((in_ch, LANES), BF16),
                 pltpu.VMEM((layers - 1, 4, 3, LANES, 2 * LANES), BF16),
                 pltpu.VMEM((4 * cols, (cols + 2) * 3 * LANES), BF16),
-                pltpu.VMEM((LANES, LANES), F32),
-                pltpu.VMEM((LANES, LANES), F32),
+                pltpu.VMEM((LANES, LANES), BF16),
+                pltpu.VMEM((LANES, LANES), BF16),
                 pltpu.VMEM(norm_first.shape, BF16),
                 pltpu.VMEM(norm_rest.shape, BF16),
                 pltpu.VMEM(bias_rest.shape, BF16),

time: 63.9 us -> 62.7 us (0.981)
  Pallas kernels: 62.3 us -> 61.1 us
    pallas_call x1, Pallas kernels: 62.3 us -> 61.1 us  [local_decode(): pl.pallas_call(functools.partial(decode_kernel, rows_n, cols_n), out_shap...]
where the time goes in v3:
time: 62.7 us; the launch traced here: 62.6 us
  Pallas kernels  61.1 us (97%)
  local copies, waits for them, and re-layouts  1.42 us (2%)
    pallas_call x1, Pallas kernels, local_decode(): pl.pallas_call(functools.partial(decode_kernel, rows_n, cols_n), out_shap...  61.1 us
    unnamed x1, local copies, waits for them, and re-layouts  1.42 us

profile of v3, /device:TPU:97, one launch (start us, length us, event | category | flops | bytes accessed | tf_op | source)
XLA Modules:
  0.0 62.6 jit_solution(1678321492185547512)
XLA Ops:
  0.0 61.1 %decode.1 = f32[2,3,8,256]{3,2,1,0:T(8,128)} custom-call(bf16[2,256,8,256]{3,2,1,0:T(8,128)(2,1)} %act_hbm.1, bf16[3,3,256,128]{3,2,1,0:T(8,128)(2,1)} %w_first_hbm.1, bf16[256,128]{1,0:T(8,128)(2,1)} %w_short_hbm.1, bf16[5,3,3,128,128]{4,3,2,1,0:T(8,128)(2,1)} %w_rest_hbm.1, bf16[2,256]{1,0:T(2,128)(2,1)} %norm_first_hbm.1, ...), custom_call_target="tpu_custom_call" | custom-call | tf_op jit(solution)/shard_map/decode/pallas_call | solution.py:385
  61.1 1.4 %copy.11 = f32[2,256,8,3]{1,2,3,0:T(8,128)} copy(f32[2,256,8,3]{1,2,3,0:T(8,128)} %bitcast.3) | data formatting | bytes 98304

commit v4 on v3

--- a/solution.py
+++ b/solution.py
@@ -19,9 +19,9 @@
     return half + half * jnp.tanh(half)
 
 
-def decode_kernel(rows_n, cols_n, act_hbm, w_first_hbm, w_short_hbm, w_rest_hbm, norm_first_hbm, norm_rest_hbm, bias_hbm, w_out_hbm, bias_out_ref, out_ref,
+def decode_kernel(rows_n, cols_n, act_hbm, w_first_hbm, w_short_hbm, w_rest_hbm, norm_first_hbm, norm_rest_hbm, bias_hbm, w_out_hbm, bias_out_hbm, out_ref,
                   raw, flat, map_in, mid_maps, hidden_maps, z_in, z_mid, short, w_first, w_short, w_rest, w_head, ones_in, ones_mid,
-                  norm_first_ref, norm_rest_ref, bias_ref, bias_rows, w_out_ref,
+                  norm_first_ref, norm_rest_ref, bias_ref, bias_rows, w_out_ref, bias_out_ref,
                   msg_in, msg_mid, got_in, got_mid, edge_in, edge_mid, halo_in, halo_mid, halo_act,
                   act_sem, weight_sem, small_sem, stat_recv, stat_send, halo_recv, halo_send):
     samples, rows, cols, in_ch = raw.shape
@@ -50,7 +50,7 @@
 
     for s in range(samples):
         pltpu.make_async_copy(act_hbm.at[s], raw.at[s], act_sem.at[s]).start()
-    small = [(norm_first_hbm, norm_first_ref), (norm_rest_hbm, norm_rest_ref), (bias_hbm, bias_ref), (w_out_hbm, w_out_ref)]
+    small = [(norm_first_hbm, norm_first_ref), (norm_rest_hbm, norm_rest_ref), (bias_hbm, bias_ref), (w_out_hbm, w_out_ref), (bias_out_hbm, bias_out_ref)]
     for at, (src, dst) in enumerate(small):
         pltpu.make_async_copy(src, dst, small_sem.at[at]).start()
     pltpu.make_async_copy(w_short_hbm, w_short, weight_sem.at[layers]).start()
@@ -126,10 +126,16 @@
         for at, move in enumerate(row_moves):
             pl.when(move[4])(lambda at=at: row_copy(k, s, at).wait_send())
 
+    def wait_rows(k, s):
+        for at, move in enumerate(row_moves):
+            pl.when(move[5])(lambda at=at: row_copy(k, s, at).wait_recv())
+
     def scales(k, s):
+        wait_rows(k, s)
         if is_first(k):
             total = msg_in[s] + jnp.sum(got_in[:, s], axis=0)
         else:
+            wait_cols(k, s)
             pltpu.make_async_copy(received(k, s), received(k, s), stat_recv.at[number(k), s]).wait()
             total = message(k, s)[...] + jnp.sum(received(k, s)[...], axis=0)
         ones = ones_in if is_first(k) else ones_mid
@@ -152,8 +158,6 @@
         return rows_out
 
     def activate_rows(k, s, scale_rows):
-        for at, move in enumerate(row_moves):
-            pl.when(move[5])(lambda at=at: row_copy(k, s, at).wait_recv())
         for part, (scale, shift) in enumerate(scale_rows):
             for side, there in ((0, "up"), (1, "down")):
                 for place in range(3):
@@ -216,7 +220,7 @@
         done = set()
         order = list(range(1, cols // 2 - 1)) + [0, cols // 2 - 1]
         for p in order:
-            if p == 0:
+            if p == 0 and is_first(k):
                 for c in range(1, cols + 1):
                     if c not in done:
                         activate(k, s, scale_rows, c)
@@ -354,13 +358,9 @@
             weights = w_head[:, blocks[0] * LANES:(blocks[-1] + 1) * LANES]
             return lax.dot_general(weights, acts, (((1,), (1,)), ((), ())), preferred_element_type=F32)
 
-        for c in range(1, cols + 1):
+        for c in range(cols + 2):
             activate(last, s, scale_rows, c)
-        rgb = product(range(3, 3 * (cols + 1)))
-        wait_cols(last, s)
-        for c in (0, cols + 1):
-            activate(last, s, scale_rows, c)
-            rgb = rgb + product(range(3 * c, 3 * c + 3))
+        rgb = product(range(3 * (cols + 2)))
         for ch in range(3):
             out_ref[s, ch] = rgb[ch * cols:(ch + 1) * cols] + bias_out_ref[:, ch:ch + 1].astype(F32)
         sent(last, s)
@@ -380,12 +380,12 @@
         halves = in_ch // LANES
         layers = w_rest.shape[0] + 1
         peers_n = rows_n * cols_n - 1
-        anywhere = pl.BlockSpec(memory_space=pl.ANY)
+        in_hbm = pl.BlockSpec(memory_space=pltpu.HBM)
         in_vmem = pl.BlockSpec(memory_space=pltpu.VMEM)
         image = pl.pallas_call(
             functools.partial(decode_kernel, rows_n, cols_n),
             out_shape=jax.ShapeDtypeStruct((samples, 3, cols, rows), F32),
-            in_specs=[anywhere] * 8 + [in_vmem],
+            in_specs=[in_hbm] * 9,
             out_specs=in_vmem,
             scratch_shapes=[
                 pltpu.VMEM((samples, rows, cols, in_ch), BF16),
@@ -407,6 +407,7 @@
                 pltpu.VMEM(bias_rest.shape, BF16),
                 pltpu.VMEM((bias_rest.shape[0], 1, LANES), F32),
                 pltpu.VMEM((3, 3, 3, LANES), BF16),
+                pltpu.VMEM((1, 3), BF16),
                 pltpu.VMEM((samples, 2 * halves, LANES), F32),
                 pltpu.VMEM((layers, samples, 2, LANES), F32),
                 pltpu.VMEM((peers_n, samples, 2 * halves, LANES), F32),
@@ -418,15 +419,15 @@
                 pltpu.VMEM((2, halves, 3 * cols, LANES), F32),
                 pltpu.SemaphoreType.DMA((samples,)),
                 pltpu.SemaphoreType.DMA((layers + 1,)),
-                pltpu.SemaphoreType.DMA((4,)),
+                pltpu.SemaphoreType.DMA((5,)),
                 pltpu.SemaphoreType.DMA((layers + 1, samples)),
                 pltpu.SemaphoreType.DMA((layers + 1, samples)),
                 pltpu.SemaphoreType.DMA((layers + 1, samples, 8)),
                 pltpu.SemaphoreType.DMA((layers + 1, samples, 8)),
             ],
-            compiler_params=pltpu.CompilerParams(collective_id=0, has_side_effects=True, vmem_limit_bytes=60 * 1024 * 1024),
+            compiler_params=pltpu.CompilerParams(collective_id=0, has_side_effects=True, vmem_limit_bytes=36 * 1024 * 1024),
             name="decode",
-        )(act_in, w_first, w_short, w_rest, norm_first, norm_rest, bias_rest, jnp.transpose(w_out, (0, 1, 3, 2)), bias_out.reshape(1, 3))
+        )(*(pltpu.with_memory_space_constraint(x, pltpu.HBM) for x in (act_in, w_first, w_short, w_rest, norm_first, norm_rest, bias_rest, jnp.transpose(w_out, (0, 1, 3, 2)), bias_out.reshape(1, 3))))
         return jnp.transpose(image, (0, 3, 2, 1))
 
     return jax.shard_map(local_decode, mesh=mesh, in_specs=(tile_spec,) + (replicated,) * 8, out_specs=tile_spec, check_vma=False)

time: 62.7 us -> 58.4 us (0.931)
  Pallas kernels: 61.1 us -> 57.7 us
  local copies, waits for them, and re-layouts: 1.42 us -> 0.62 us
    pallas_call x1, Pallas kernels: 61.1 us -> 57.7 us  [local_decode(): pl.pallas_call(functools.partial(decode_kernel, rows_n, cols_n), out_shap...]
    unnamed x1, local copies, waits for them, and re-layouts: 1.42 us -> 0.62 us
where the time goes in v4:
time: 58.4 us; the launch traced here: 58.3 us
  Pallas kernels  57.7 us (99%)
  local copies, waits for them, and re-layouts  0.62 us (1%)
    pallas_call x1, Pallas kernels, local_decode(): pl.pallas_call(functools.partial(decode_kernel, rows_n, cols_n), out_shap...  57.7 us

profile of v4, /device:TPU:97, one launch (start us, length us, event | category | flops | bytes accessed | tf_op | source)
XLA Modules:
  0.0 58.3 jit_solution(2293563361651426250)
XLA Ops:
  0.0 57.7 %decode.1 = f32[2,3,8,256]{3,2,1,0:T(8,128)S(1)} custom-call(bf16[2,256,8,256]{3,2,1,0:T(8,128)(2,1)} %act_hbm.1, bf16[3,3,256,128]{3,2,1,0:T(8,128)(2,1)} %w_first_hbm.1, bf16[256,128]{1,0:T(8,128)(2,1)} %w_short_hbm.1, bf16[5,3,3,128,128]{4,3,2,1,0:T(8,128)(2,1)} %w_rest_hbm.1, bf16[2,256]{1,0:T(2,128)(2,1)} %norm_first_hbm.1, ...), custom_call_target="tpu_custom_call" | custom-call | tf_op jit(solution)/shard_map/decode/pallas_call | solution.py:385
  57.7 0.6 %copy.11 = f32[2,256,8,3]{1,2,3,0:T(8,128)} copy(f32[2,256,8,3]{1,2,3,0:T(8,128)S(1)} %bitcast.3) | data formatting | bytes 98304

commit v5 on v4

--- a/solution.py
+++ b/solution.py
@@ -20,7 +20,7 @@
 
 
 def decode_kernel(rows_n, cols_n, act_hbm, w_first_hbm, w_short_hbm, w_rest_hbm, norm_first_hbm, norm_rest_hbm, bias_hbm, w_out_hbm, bias_out_hbm, out_ref,
-                  raw, flat, map_in, mid_maps, hidden_maps, z_in, z_mid, short, w_first, w_short, w_rest, w_head, ones_in, ones_mid,
+                  raw, flat, map_in, mid_maps, hidden_maps, z_in, z_mid, short, w_first, w_short, w_rest, w_head, z_edge, ones_in, ones_mid,
                   norm_first_ref, norm_rest_ref, bias_ref, bias_rows, w_out_ref, bias_out_ref,
                   msg_in, msg_mid, got_in, got_mid, edge_in, edge_mid, halo_in, halo_mid, halo_act,
                   act_sem, weight_sem, small_sem, stat_recv, stat_send, halo_recv, halo_send):
@@ -150,8 +150,8 @@
         rows_out = []
         for part in range(parts):
             norm = (norm_first_ref[:, part * LANES:(part + 1) * LANES] if is_first(k) else norm_rest_ref[number(k) - 1]).astype(F32)
-            mean = total[part:part + 1] / count
-            square = total[parts + part:parts + part + 1] / count
+            mean = total[part:part + 1] * (1.0 / count)
+            square = total[parts + part:parts + part + 1] * (1.0 / count)
             scale = lax.rsqrt(square - mean * mean + GN_EPS) * norm[0:1]
             shift = norm[1:2] - mean * scale
             rows_out.append((0.5 * scale, 0.5 * shift))
@@ -316,15 +316,15 @@
     col_id = lax.broadcasted_iota(jnp.int32, (cols, LANES), 0)
 
     def head_block(j, _):
+        blocks = []
         for dr in range(3):
-            blocks = []
             for ch in range(3):
                 block = jnp.zeros((cols, LANES), F32)
                 for dc in range(3):
                     block = jnp.where(col_id == j - dc, w_out_ref[dr, dc, ch:ch + 1, :].astype(F32), block)
                 blocks.append(block)
-            blocks.append(jnp.zeros((cols, LANES), F32))
-            w_head[:, pl.ds(pl.multiple_of((j * 3 + dr) * LANES, LANES), LANES)] = jnp.concatenate(blocks, axis=0).astype(BF16)
+        blocks.append(jnp.zeros((cols, LANES), F32))
+        w_head[:, pl.ds(pl.multiple_of(j * LANES, LANES), LANES)] = jnp.concatenate(blocks, axis=0).astype(BF16)
         return 0
 
     lax.fori_loop(0, cols + 2, head_block, 0)
@@ -353,14 +353,26 @@
         scale_rows = scales(last, s)
         activate_rows(last, s, scale_rows)
 
-        def product(blocks):
-            acts = jnp.concatenate([z_mid[i] for i in blocks], axis=1)
-            weights = w_head[:, blocks[0] * LANES:(blocks[-1] + 1) * LANES]
-            return lax.dot_general(weights, acts, (((1,), (1,)), ((), ())), preferred_element_type=F32)
-
+        scale, shift = scale_rows[0]
         for c in range(cols + 2):
-            activate(last, s, scale_rows, c)
-        rgb = product(range(3 * (cols + 2)))
+            act = half_silu(tile(last, s, c)[...].astype(F32) * scale + shift)
+            if c in (0, cols + 1):
+                act = jnp.where(has["left" if c == 0 else "right"], act, 0.0)
+            z_mid[c] = act.astype(BF16)
+            at = cols - 1 + c
+            ends = [halo_act[side, 0, at:at + 1, :] for side in range(2)] + [jnp.zeros((14, LANES), F32)]
+            z_edge[c] = jnp.concatenate(ends, axis=0).astype(BF16)
+
+        def product(ref):
+            acts = jnp.concatenate([ref[c] for c in range(cols + 2)], axis=1)
+            return lax.dot_general(w_head[...], acts, (((1,), (1,)), ((), ())), preferred_element_type=F32)
+
+        taps = product(z_mid)
+        ends = product(z_edge)
+        part = 3 * cols
+        above = jnp.concatenate([ends[:part, 0:1], taps[:part, :-1]], axis=1)
+        below = jnp.concatenate([taps[2 * part:3 * part, 1:], ends[2 * part:3 * part, 1:2]], axis=1)
+        rgb = above + taps[part:2 * part] + below
         for ch in range(3):
             out_ref[s, ch] = rgb[ch * cols:(ch + 1) * cols] + bias_out_ref[:, ch:ch + 1].astype(F32)
         sent(last, s)
@@ -399,7 +411,8 @@
                 pltpu.VMEM((4, 3, in_ch, 2 * LANES), BF16),
                 pltpu.VMEM((in_ch, LANES), BF16),
                 pltpu.VMEM((layers - 1, 4, 3, LANES, 2 * LANES), BF16),
-                pltpu.VMEM((4 * cols, (cols + 2) * 3 * LANES), BF16),
+                pltpu.VMEM((10 * cols, (cols + 2) * LANES), BF16),
+                pltpu.VMEM((cols + 2, 16, LANES), BF16),
                 pltpu.VMEM((LANES, LANES), BF16),
                 pltpu.VMEM((LANES, LANES), BF16),
                 pltpu.VMEM(norm_first.shape, BF16),

time: 58.4 us -> 58.1 us (level)
  no operation moved by 1% of the time
where the time goes in v5:
time: 58.1 us
  Pallas kernels  57.4 us (99%)
  local copies, waits for them, and re-layouts  0.62 us (1%)
    pallas_call x1, Pallas kernels, local_decode(): pl.pallas_call(functools.partial(decode_kernel, rows_n, cols_n), out_shap...  57.4 us

profile of v5, /device:TPU:97, one launch (start us, length us, event | category | flops | bytes accessed | tf_op | source)
XLA Modules:
  0.0 58.1 jit_solution(9318588835396772979)
XLA Ops:
  0.0 57.4 %decode.1 = f32[2,3,8,256]{3,2,1,0:T(8,128)S(1)} custom-call(bf16[2,256,8,256]{3,2,1,0:T(8,128)(2,1)} %act_hbm.1, bf16[3,3,256,128]{3,2,1,0:T(8,128)(2,1)} %w_first_hbm.1, bf16[256,128]{1,0:T(8,128)(2,1)} %w_short_hbm.1, bf16[5,3,3,128,128]{4,3,2,1,0:T(8,128)(2,1)} %w_rest_hbm.1, bf16[2,256]{1,0:T(2,128)(2,1)} %norm_first_hbm.1, ...), custom_call_target="tpu_custom_call" | custom-call | tf_op jit(solution)/shard_map/decode/pallas_call | solution.py:397
  57.4 0.6 %copy.11 = f32[2,256,8,3]{1,2,3,0:T(8,128)} copy(f32[2,256,8,3]{1,2,3,0:T(8,128)S(1)} %bitcast.3) | data formatting | bytes 98304

commit v6 on v5

--- a/solution.py
+++ b/solution.py
@@ -194,8 +194,8 @@
         edge = edges(later, s)
 
         def pair(p, sums):
-            lhs = jnp.concatenate([z[2 * p * depth + i] for i in range(4 * depth)], axis=1)
-            acc = jnp.dot(lhs, weights, preferred_element_type=F32)
+            acc = jnp.concatenate([jnp.dot(jnp.concatenate([z[2 * p * depth + i, lo:lo + rows // 2] for i in range(4 * depth)], axis=1), weights, preferred_element_type=F32)
+                                   for lo in (0, rows // 2)], axis=0)
             sum_one, sum_two = sums
             for o in range(2):
                 c = 2 * p + o

time: 58.1 us -> 58 us (level)
  no operation moved by 1% of the time
where the time goes in v6:
time: 58 us; the launch traced here: 57.9 us
  Pallas kernels  57.3 us (99%)
  local copies, waits for them, and re-layouts  0.62 us (1%)
    pallas_call x1, Pallas kernels, local_decode(): pl.pallas_call(functools.partial(decode_kernel, rows_n, cols_n), out_shap...  57.3 us

profile of v6, /device:TPU:97, one launch (start us, length us, event | category | flops | bytes accessed | tf_op | source)
XLA Modules:
  0.0 57.9 jit_solution(1347634696226217720)
XLA Ops:
  0.0 57.3 %decode.1 = f32[2,3,8,256]{3,2,1,0:T(8,128)S(1)} custom-call(bf16[2,256,8,256]{3,2,1,0:T(8,128)(2,1)} %act_hbm.1, bf16[3,3,256,128]{3,2,1,0:T(8,128)(2,1)} %w_first_hbm.1, bf16[256,128]{1,0:T(8,128)(2,1)} %w_short_hbm.1, bf16[5,3,3,128,128]{4,3,2,1,0:T(8,128)(2,1)} %w_rest_hbm.1, bf16[2,256]{1,0:T(2,128)(2,1)} %norm_first_hbm.1, ...), custom_call_target="tpu_custom_call" | custom-call | tf_op jit(solution)/shard_map/decode/pallas_call | solution.py:397
  57.3 0.6 %copy.11 = f32[2,256,8,3]{1,2,3,0:T(8,128)} copy(f32[2,256,8,3]{1,2,3,0:T(8,128)S(1)} %bitcast.3) | data formatting | bytes 98304
